TPU v7x, 32 devices: a whole 2x2x4 slice. The times are simulated.
32 devices in a mesh: dp: 4 (over y, x), seq: 8 (over z, core).
Axes of the slice: x: 2, y: 2, z: 4, core: 2. Of those that a mesh axis runs over, the one named last changes fastest.
Arguments:
- tokens: bfloat16 [8, 1024, 2048], P('dp', 'seq'), may hold values from -6 to 6
- cotangent: bfloat16 [8, 1024, 2048], P('dp', 'seq'), may hold values from -6 to 6
- w_query: bfloat16 [2048, 2048], P(('dp', 'seq')), may hold values from -0.1875 to 0.1875
- w_key: bfloat16 [2048, 256], P(('dp', 'seq')), may hold values from -0.1875 to 0.1875
- w_value: bfloat16 [2048, 256], P(('dp', 'seq')), may hold values from -0.125 to 0.125
- w_output: bfloat16 [2048, 2048], P(('dp', 'seq')), may hold values from -0.75 to 0.75
- gain_attn: bfloat16 [2048], P(('dp', 'seq')), may hold values from 0.5 to 1.5
- w_gate: bfloat16 [2048, 5632], P(('dp', 'seq')), may hold values from -0.125 to 0.125
- w_up: bfloat16 [2048, 5632], P(('dp', 'seq')), may hold values from -0.125 to 0.125
- w_down: bfloat16 [5632, 2048], P(('dp', 'seq')), may hold values from -0.109375 to 0.109375
- gain_mlp: bfloat16 [2048], P(('dp', 'seq')), may hold values from 0.5 to 1.5
- span_start: int32 [8, 2], P('dp'), may hold values from 0 to 768, as said below
- span_len: int32 [8, 2], P('dp'), may hold values from 64 to 256
Outputs:
- layer_out: bfloat16 [8, 1024, 2048], P('dp', 'seq')
- input_grad: bfloat16 [8, 1024, 2048], P('dp', 'seq')
- grad_query: float32 [2048, 2048], P(('dp', 'seq'))
- grad_key: float32 [2048, 256], P(('dp', 'seq'))
- grad_value: float32 [2048, 256], P(('dp', 'seq'))
- grad_output: float32 [2048, 2048], P(('dp', 'seq'))
- grad_gain_attn: float32 [2048], P(('dp', 'seq'))
- grad_gate: float32 [2048, 5632], P(('dp', 'seq'))
- grad_up: float32 [2048, 5632], P(('dp', 'seq'))
- grad_down: float32 [5632, 2048], P(('dp', 'seq'))
- grad_gain_mlp: float32 [2048], P(('dp', 'seq'))
Inputs may be any that keep to these rules, and one draw needn't show every extreme that they name: `span_start`: the k-th picture of a sequence starts within positions k * 512 to (k + 1) * 512 - 256, so pictures never intersect.
All inputs are finite; a program needn't handle non-finite values.
Results may differ from a plain program's by a relative error of at most 0.02.
Values may be sent and summed in bfloat16 or wider, within the bound.
A program may use at most 384 MiB of HBM per device.

v0:
```python
import math

import jax
import jax.numpy as jnp
from jax import lax
from jax.sharding import PartitionSpec as P

H = 32
KVH = 4
HD = 64
MICRO = 2


epsilon = 1e-05
masked_value = -1e30
rope_base = 10000.0


def rope_tables(positions, half_width):
    frequency = rope_base ** (-jnp.arange(half_width, dtype=jnp.float32) / half_width)
    angles = positions.astype(jnp.float32)[:, None] * frequency[None, :]
    return (jnp.cos(angles), jnp.sin(angles))


def rotate(values, cosine, sine):
    half_width = values.shape[-1] // 2
    first_half = values[..., :half_width]
    second_half = values[..., half_width:]
    cosine_rows = cosine[:, None, :]
    sine_rows = sine[:, None, :]
    return jnp.concatenate(
        [
            first_half * cosine_rows - second_half * sine_rows,
            second_half * cosine_rows + first_half * sine_rows,
        ],
        axis=-1,
    )


def unrotate(values, cosine, sine):
    half_width = values.shape[-1] // 2
    first_half = values[..., :half_width]
    second_half = values[..., half_width:]
    cosine_rows = cosine[:, None, :]
    sine_rows = sine[:, None, :]
    return jnp.concatenate(
        [
            first_half * cosine_rows + second_half * sine_rows,
            second_half * cosine_rows - first_half * sine_rows,
        ],
        axis=-1,
    )


def picture_of(positions, starts, lengths):
    inside = (positions[..., None, :] >= starts[..., :, None]) & (
        positions[..., None, :] < (starts + lengths)[..., :, None]
    )
    labels = jnp.arange(1, starts.shape[-1] + 1, dtype=jnp.int32)
    return jnp.sum(jnp.where(inside, labels[:, None], 0), axis=-2) - 1


def rms_scale(values):
    return lax.rsqrt(jnp.mean(values * values, axis=-1, keepdims=True) + epsilon)


def rms_back(grad_normed, values, inverse, gain):
    scaled_grad = grad_normed * gain
    unit_rows = values * inverse
    grad_values = inverse * (
        scaled_grad - unit_rows * jnp.mean(scaled_grad * unit_rows, axis=-1, keepdims=True)
    )
    return (grad_values, jnp.sum(grad_normed * unit_rows, axis=0))


def key_block(block_index, block_width, key_all, value_all, all_pic):
    key_start = block_index * block_width
    key_part = lax.dynamic_slice_in_dim(key_all, key_start, block_width, 1)
    value_part = lax.dynamic_slice_in_dim(value_all, key_start, block_width, 1)
    key_pos = key_start + jnp.arange(block_width, dtype=jnp.int32)
    key_pic = lax.dynamic_slice_in_dim(all_pic, key_start, block_width, 1)
    return (key_part, value_part, key_pos, key_pic, key_start)


def masked_scores(queries, key_part, local_pos, local_pic, key_pos, key_pic):
    score_scale = 1.0 / math.sqrt(HD)
    scores = (
        jnp.einsum("scgrd,skcd->scgrk", queries, key_part, preferred_element_type=jnp.float32)
        * score_scale
    )
    allowed = (key_pos[None, None, :] <= local_pos[None, :, None]) | (
        local_pic[:, :, None] == key_pic[:, None, :]
    ) & (local_pic[:, :, None] >= 0)
    return jnp.where(allowed[:, None, None], scores, masked_value)


def attend(queries, key_all, value_all, local_pos, local_pic, all_pic):
    block_width = min(256, key_all.shape[1])
    indices = jnp.arange(key_all.shape[1] // block_width, dtype=jnp.int32)

    def first_pass(running, block_index):
        row_top, row_total = running
        key_part, value_part, key_pos, key_pic, key_start = key_block(
            block_index, block_width, key_all, value_all, all_pic
        )
        scores = masked_scores(queries, key_part, local_pos, local_pic, key_pos, key_pic)
        new_top = jnp.maximum(row_top, jnp.max(scores, axis=-1))
        row_total = row_total * jnp.exp(row_top - new_top) + jnp.sum(
            jnp.exp(scores - new_top[..., None]), axis=-1
        )
        return ((new_top, row_total), None)

    row_shape = queries.shape[:-1]
    (row_top, row_total), unused = lax.scan(
        first_pass,
        (jnp.full(row_shape, masked_value, jnp.float32), jnp.zeros(row_shape, jnp.float32)),
        indices,
    )
    log_total = row_top + jnp.log(row_total)

    def second_pass(mixture, block_index):
        key_part, value_part, key_pos, key_pic, key_start = key_block(
            block_index, block_width, key_all, value_all, all_pic
        )
        scores = masked_scores(queries, key_part, local_pos, local_pic, key_pos, key_pic)
        weights_low = jnp.exp(scores - log_total[..., None]).astype(jnp.bfloat16)
        return (
            mixture
            + jnp.einsum(
                "scgrk,skcd->scgrd", weights_low, value_part, preferred_element_type=jnp.float32
            ),
            None,
        )

    mixture, unused = lax.scan(second_pass, jnp.zeros(queries.shape, jnp.float32), indices)
    return (log_total, mixture)


def attend_back(
    queries, key_all, value_all, local_pos, local_pic, all_pic, log_total, grad_mix, delta
):
    block_width = min(256, key_all.shape[1])
    indices = jnp.arange(key_all.shape[1] // block_width, dtype=jnp.int32)
    score_scale = 1.0 / math.sqrt(HD)

    def step_back(running, block_index):
        grad_query, grad_key_all, grad_value_all = running
        key_part, value_part, key_pos, key_pic, key_start = key_block(
            block_index, block_width, key_all, value_all, all_pic
        )
        scores = masked_scores(queries, key_part, local_pos, local_pic, key_pos, key_pic)
        probability = jnp.exp(scores - log_total[..., None])
        grad_value_part = jnp.einsum(
            "scgrk,scgrd->skcd",
            probability.astype(jnp.bfloat16),
            grad_mix,
            preferred_element_type=jnp.float32,
        )
        grad_prob = jnp.einsum(
            "scgrd,skcd->scgrk", grad_mix, value_part, preferred_element_type=jnp.float32
        )
        grad_scores = (probability * (grad_prob - delta[..., None])).astype(jnp.bfloat16)
        grad_query = (
            grad_query
            + jnp.einsum(
                "scgrk,skcd->scgrd", grad_scores, key_part, preferred_element_type=jnp.float32
            )
            * score_scale
        )
        grad_key_part = (
            jnp.einsum(
                "scgrk,scgrd->skcd", grad_scores, queries, preferred_element_type=jnp.float32
            )
            * score_scale
        )
        grad_key_all = lax.dynamic_update_slice_in_dim(grad_key_all, grad_key_part, key_start, 1)
        grad_value_all = lax.dynamic_update_slice_in_dim(
            grad_value_all, grad_value_part, key_start, 1
        )
        return ((grad_query, grad_key_all, grad_value_all), None)

    initial = (
        jnp.zeros(queries.shape, jnp.float32),
        jnp.zeros(key_all.shape, jnp.float32),
        jnp.zeros(value_all.shape, jnp.float32),
    )
    result, unused = lax.scan(step_back, initial, indices)
    return result


def layer_forward(
    seq_tokens, seq_starts, seq_lengths, attention_set, feed_set, local_pos, all_pos, cosine, sine
):
    w_query, w_key, w_value, w_output, gain_attn = attention_set
    w_gate, w_up, w_down, gain_mlp = feed_set
    seq_count, row_count, model_width = seq_tokens.shape
    group_size = H // KVH
    inputs = seq_tokens.astype(jnp.float32).reshape(seq_count * row_count, model_width)
    inverse_attn = rms_scale(inputs)
    normed = (inputs * inverse_attn * gain_attn.astype(jnp.float32)).astype(jnp.bfloat16)
    query_pre = jnp.dot(normed, w_query, preferred_element_type=jnp.float32)
    key_pre = jnp.dot(normed, w_key, preferred_element_type=jnp.float32)
    value_pre = jnp.dot(normed, w_value, preferred_element_type=jnp.float32)
    queries = rotate(query_pre.reshape(seq_count, row_count, H, HD), cosine, sine).astype(
        jnp.bfloat16
    )
    queries = queries.reshape(seq_count, row_count, KVH, group_size, HD).transpose(0, 2, 3, 1, 4)
    own_keys = (
        rotate(key_pre.reshape(seq_count, row_count, KVH, HD), cosine, sine)
        .astype(jnp.bfloat16)
        .reshape(seq_count, row_count, KVH * HD)
    )
    own_values = value_pre.astype(jnp.bfloat16).reshape(seq_count, row_count, KVH * HD)
    key_all, value_all = (
        lax.all_gather(own_keys, "seq", axis=1, tiled=True),
        lax.all_gather(own_values, "seq", axis=1, tiled=True),
    )
    seq_length = key_all.shape[1]
    key_all = key_all.reshape(seq_count, seq_length, KVH, HD)
    value_all = value_all.reshape(seq_count, seq_length, KVH, HD)
    local_pic = picture_of(local_pos, seq_starts, seq_lengths)
    all_pic = picture_of(all_pos, seq_starts, seq_lengths)
    log_total, mixture = attend(queries, key_all, value_all, local_pos, local_pic, all_pic)
    attended = (
        mixture.astype(jnp.bfloat16)
        .transpose(0, 3, 1, 2, 4)
        .reshape(seq_count * row_count, model_width)
    )
    middle = inputs + jnp.dot(attended, w_output, preferred_element_type=jnp.float32)
    inverse_mlp = rms_scale(middle)
    normed_mid = (middle * inverse_mlp * gain_mlp.astype(jnp.float32)).astype(jnp.bfloat16)
    gate_pre = jnp.dot(normed_mid, w_gate, preferred_element_type=jnp.float32)
    up_pre = jnp.dot(normed_mid, w_up, preferred_element_type=jnp.float32)
    hidden = (gate_pre * jax.nn.sigmoid(gate_pre) * up_pre).astype(jnp.bfloat16)
    layer_out = (middle + jnp.dot(hidden, w_down, preferred_element_type=jnp.float32)).astype(
        jnp.bfloat16
    )
    stored = (
        inputs,
        inverse_attn,
        normed,
        queries,
        key_all,
        value_all,
        local_pic,
        all_pic,
        log_total,
        mixture,
        attended,
        middle,
        inverse_mlp,
        normed_mid,
        gate_pre,
        up_pre,
        hidden,
    )
    return (layer_out.reshape(seq_count, row_count, model_width), stored)


def layer_backward(seq_grad, stored, attention_set, feed_set, local_pos, cosine, sine):
    w_query, w_key, w_value, w_output, gain_attn = attention_set
    w_gate, w_up, w_down, gain_mlp = feed_set
    (
        inputs,
        inverse_attn,
        normed,
        queries,
        key_all,
        value_all,
        local_pic,
        all_pic,
        log_total,
        mixture,
        attended,
        middle,
        inverse_mlp,
        normed_mid,
        gate_pre,
        up_pre,
        hidden,
    ) = stored
    seq_count, row_count, model_width = seq_grad.shape
    token_count = seq_count * row_count
    grad_low = seq_grad.reshape(token_count, model_width)
    grad_full = grad_low.astype(jnp.float32)
    weight_down = jnp.einsum("nf,nd->fd", hidden, grad_low, preferred_element_type=jnp.float32)
    grad_hidden = (
        jnp.einsum("nd,fd->nf", grad_low, w_down, preferred_element_type=jnp.float32)
        .astype(jnp.bfloat16)
        .astype(jnp.float32)
    )
    sigmoid_gate = jax.nn.sigmoid(gate_pre)
    grad_gate = (
        grad_hidden * up_pre * sigmoid_gate * (1.0 + gate_pre * (1.0 - sigmoid_gate))
    ).astype(jnp.bfloat16)
    grad_up = (grad_hidden * gate_pre * sigmoid_gate).astype(jnp.bfloat16)
    weight_gate = jnp.einsum("nd,nf->df", normed_mid, grad_gate, preferred_element_type=jnp.float32)
    weight_up = jnp.einsum("nd,nf->df", normed_mid, grad_up, preferred_element_type=jnp.float32)
    grad_normed_mid = jnp.einsum(
        "nf,df->nd", grad_gate, w_gate, preferred_element_type=jnp.float32
    ) + jnp.einsum("nf,df->nd", grad_up, w_up, preferred_element_type=jnp.float32)
    grad_middle_norm, weight_gain_mlp = rms_back(
        grad_normed_mid, middle, inverse_mlp, gain_mlp.astype(jnp.float32)
    )
    grad_middle = grad_full + grad_middle_norm
    grad_middle_low = grad_middle.astype(jnp.bfloat16)
    weight_output = jnp.einsum(
        "ne,nd->ed", attended, grad_middle_low, preferred_element_type=jnp.float32
    )
    grad_mix = jnp.einsum(
        "nd,ed->ne", grad_middle_low, w_output, preferred_element_type=jnp.float32
    ).astype(jnp.bfloat16)
    grad_mix = grad_mix.reshape(seq_count, row_count, KVH, H // KVH, HD).transpose(0, 2, 3, 1, 4)
    delta = jnp.sum(grad_mix.astype(jnp.float32) * mixture, axis=-1)
    grad_query, grad_key_all, grad_value_all = attend_back(
        queries, key_all, value_all, local_pos, local_pic, all_pic, log_total, grad_mix, delta
    )
    seq_length = key_all.shape[1]
    grad_key_own, grad_value_own = (
        lax.psum_scatter(
            grad_key_all.reshape(seq_count, seq_length, KVH * HD).astype(jnp.bfloat16),
            "seq",
            scatter_dimension=1,
            tiled=True,
        ).astype(jnp.float32),
        lax.psum_scatter(
            grad_value_all.reshape(seq_count, seq_length, KVH * HD).astype(jnp.bfloat16),
            "seq",
            scatter_dimension=1,
            tiled=True,
        ).astype(jnp.float32),
    )
    grad_query_pre = (
        unrotate(
            grad_query.transpose(0, 3, 1, 2, 4).reshape(seq_count, row_count, H, HD), cosine, sine
        )
        .astype(jnp.bfloat16)
        .reshape(token_count, model_width)
    )
    grad_key_pre = (
        unrotate(grad_key_own.reshape(seq_count, row_count, KVH, HD), cosine, sine)
        .astype(jnp.bfloat16)
        .reshape(token_count, KVH * HD)
    )
    grad_value_pre = grad_value_own.astype(jnp.bfloat16).reshape(token_count, KVH * HD)
    weight_query = jnp.einsum(
        "nd,ne->de", normed, grad_query_pre, preferred_element_type=jnp.float32
    )
    weight_key = jnp.einsum("nd,ne->de", normed, grad_key_pre, preferred_element_type=jnp.float32)
    weight_value = jnp.einsum(
        "nd,ne->de", normed, grad_value_pre, preferred_element_type=jnp.float32
    )
    grad_normed = jnp.einsum(
        "ne,de->nd", grad_query_pre, w_query, preferred_element_type=jnp.float32
    )
    grad_normed = grad_normed + jnp.einsum(
        "ne,de->nd", grad_key_pre, w_key, preferred_element_type=jnp.float32
    )
    grad_normed = grad_normed + jnp.einsum(
        "ne,de->nd", grad_value_pre, w_value, preferred_element_type=jnp.float32
    )
    grad_input_norm, weight_gain_attn = rms_back(
        grad_normed, inputs, inverse_attn, gain_attn.astype(jnp.float32)
    )
    input_grad = (
        (grad_middle + grad_input_norm)
        .astype(jnp.bfloat16)
        .reshape(seq_count, row_count, model_width)
    )
    return (
        input_grad,
        (
            weight_query,
            weight_key,
            weight_value,
            weight_output,
            weight_gain_attn,
            weight_gate,
            weight_up,
            weight_down,
            weight_gain_mlp,
        ),
    )


def local(
    tokens,
    cotangent,
    w_query,
    w_key,
    w_value,
    w_output,
    gain_attn,
    w_gate,
    w_up,
    w_down,
    gain_mlp,
    span_start,
    span_len,
):
    row_count = tokens.shape[1]
    seq_length = row_count * lax.axis_size("seq")
    local_pos = lax.axis_index("seq") * row_count + jnp.arange(row_count, dtype=jnp.int32)
    all_pos = jnp.arange(seq_length, dtype=jnp.int32)
    cosine, sine = rope_tables(local_pos, HD // 2)
    per_micro = tokens.shape[0] // MICRO
    output_pieces = []
    input_pieces = []
    totals = None
    for micro_index in range(MICRO):
        first_seq = micro_index * per_micro
        seq_tokens = tokens[first_seq : first_seq + per_micro]
        seq_grad = cotangent[first_seq : first_seq + per_micro]
        seq_starts = span_start[first_seq : first_seq + per_micro]
        seq_lengths = span_len[first_seq : first_seq + per_micro]
        attention_set = (
            lax.all_gather(w_query, ("dp", "seq"), axis=0, tiled=True),
            lax.all_gather(w_key, ("dp", "seq"), axis=0, tiled=True),
            lax.all_gather(w_value, ("dp", "seq"), axis=0, tiled=True),
            lax.all_gather(w_output, ("dp", "seq"), axis=0, tiled=True),
            lax.all_gather(gain_attn, ("dp", "seq"), axis=0, tiled=True),
        )
        feed_set = (
            lax.all_gather(w_gate, ("dp", "seq"), axis=0, tiled=True),
            lax.all_gather(w_up, ("dp", "seq"), axis=0, tiled=True),
            lax.all_gather(w_down, ("dp", "seq"), axis=0, tiled=True),
            lax.all_gather(gain_mlp, ("dp", "seq"), axis=0, tiled=True),
        )
        layer_out, stored = layer_forward(
            seq_tokens,
            seq_starts,
            seq_lengths,
            attention_set,
            feed_set,
            local_pos,
            all_pos,
            cosine,
            sine,
        )
        back_attention = (
            lax.all_gather(w_query, ("dp", "seq"), axis=0, tiled=True),
            lax.all_gather(w_key, ("dp", "seq"), axis=0, tiled=True),
            lax.all_gather(w_value, ("dp", "seq"), axis=0, tiled=True),
            lax.all_gather(w_output, ("dp", "seq"), axis=0, tiled=True),
            lax.all_gather(gain_attn, ("dp", "seq"), axis=0, tiled=True),
        )
        back_feed = (
            lax.all_gather(w_gate, ("dp", "seq"), axis=0, tiled=True),
            lax.all_gather(w_up, ("dp", "seq"), axis=0, tiled=True),
            lax.all_gather(w_down, ("dp", "seq"), axis=0, tiled=True),
            lax.all_gather(gain_mlp, ("dp", "seq"), axis=0, tiled=True),
        )
        input_grad, gradients = layer_backward(
            seq_grad, stored, back_attention, back_feed, local_pos, cosine, sine
        )
        if totals is None:
            totals = tuple(gradients)
        else:
            totals = tuple((running + extra for running, extra in zip(totals, gradients)))
        output_pieces.append(layer_out)
        input_pieces.append(input_grad)
    totals = (
        lax.psum_scatter(totals[0], ("dp", "seq"), scatter_dimension=0, tiled=True),
        lax.psum_scatter(totals[1], ("dp", "seq"), scatter_dimension=0, tiled=True),
        lax.psum_scatter(totals[2], ("dp", "seq"), scatter_dimension=0, tiled=True),
        lax.psum_scatter(totals[3], ("dp", "seq"), scatter_dimension=0, tiled=True),
        lax.psum_scatter(totals[4], ("dp", "seq"), scatter_dimension=0, tiled=True),
        lax.psum_scatter(totals[5], ("dp", "seq"), scatter_dimension=0, tiled=True),
        lax.psum_scatter(totals[6], ("dp", "seq"), scatter_dimension=0, tiled=True),
        lax.psum_scatter(totals[7], ("dp", "seq"), scatter_dimension=0, tiled=True),
        lax.psum_scatter(totals[8], ("dp", "seq"), scatter_dimension=0, tiled=True),
    )
    return (
        jnp.concatenate(output_pieces, axis=0),
        jnp.concatenate(input_pieces, axis=0),
        totals[0],
        totals[1],
        totals[2],
        totals[3],
        totals[4],
        totals[5],
        totals[6],
        totals[7],
        totals[8],
    )


def solution(mesh):
    return jax.shard_map(
        local,
        mesh=mesh,
        in_specs=(
            P("dp", "seq", None),
            P("dp", "seq", None),
            P(("dp", "seq"), None),
            P(("dp", "seq"), None),
            P(("dp", "seq"), None),
            P(("dp", "seq"), None),
            P(("dp", "seq")),
            P(("dp", "seq"), None),
            P(("dp", "seq"), None),
            P(("dp", "seq"), None),
            P(("dp", "seq")),
            P("dp", None),
            P("dp", None),
        ),
        out_specs=(
            P("dp", "seq", None),
            P("dp", "seq", None),
            P(("dp", "seq"), None),
            P(("dp", "seq"), None),
            P(("dp", "seq"), None),
            P(("dp", "seq"), None),
            P(("dp", "seq")),
            P(("dp", "seq"), None),
            P(("dp", "seq"), None),
            P(("dp", "seq"), None),
            P(("dp", "seq")),
        ),
        check_vma=False,
    )
```

profile of v0, /device:TPU:0, one launch (start us, length us, event | category | flops | bytes accessed | tf_op | source)
XLA Modules:
  0.0 3193.1 jit_solution(11501952690748943144)
XLA Ops:
  13.7 42.1 %all-reduce.5 = (bf16[2048]{0:T(1024)(128)(2,1)S(1)}, bf16[2048]{0:T(1024)(128)(2,1)S(1)}) all-reduce(bf16[2048]{0:T(1024)(128)(2,1)S(1)} %dynamic-update-slice, bf16[2048]{0:T(1024)(128)(2,1)S(1)} %dynamic-update-slice.1), channel_id=1, replica_groups=mesh['dp'=4,'seq'=8] {'dp','seq'}, use_global_device_ids=true, to_apply=%add | all-reduce | flops 4096 | bytes 16384
  58.6 9.1 all-gather.10.cloned.1.call-done
  69.2 54.3 %all-gather.14.cloned.1.call-done = bf16[2048,256]{1,0:T(8,128)(2,1)} async-done(((bf16[64,256]{1,0:T(8,128)(2,1)}), bf16[2048,256]{1,0:T(8,128)(2,1)}) %all-gather.14.cloned.1.call-update) | async-done | bytes 1048592 | tf_op jit(solution)/shard_map/all_gather | solution.py:419
  125.1 14.8 all-gather.1
  142.4 15.1 all-gather
  159.7 16.0 all_gather.37
  175.7 18.8 all_gather.28
  194.5 12.2 all-gather.12.cloned.1.call-done
  206.7 12.0 copy.81
  218.7 6.0 convolution_bitcast_fusion.3
  228.3 29.1 while.80
  239.7 3.1 exponential_reduce_fusion.5
  257.5 20.4 while.81
  258.9 3.3 fusion.345
  263.7 3.7 fusion.345
  268.9 3.7 fusion.345
  274.0 3.8 fusion.345
  281.5 29.2 while.78
  292.9 3.1 exponential_reduce_fusion.4
  307.5 3.1 exponential_reduce_fusion.4
  310.7 20.8 while.79
  312.1 3.3 fusion.340
  316.9 3.7 fusion.340
  322.1 3.8 fusion.340
  327.3 3.8 fusion.340
  333.0 5.0 multiply_reduce_fusion.7
  341.7 89.7 %all-gather.18.cloned.1.call-done = bf16[2048,5632]{1,0:T(8,128)(2,1)} async-done(((bf16[64,5632]{1,0:T(8,128)(2,1)}), bf16[2048,5632]{1,0:T(8,128)(2,1)}) %all-gather.18.cloned.1.call-update) | async-done | bytes 23068688 | tf_op jit(solution)/shard_map/all_gather | solution.py:424
  431.4 12.3 fusion.222
  443.7 132.5 %all-gather.20.cloned.1.call-done = bf16[2048,5632]{1,0:T(8,128)(2,1)} async-done(((bf16[64,5632]{1,0:T(8,128)(2,1)}), bf16[2048,5632]{1,0:T(8,128)(2,1)}) %all-gather.20.cloned.1.call-update) | async-done | bytes 23068688 | tf_op jit(solution)/shard_map/all_gather | solution.py:425
  576.2 12.4 fusion.223
  588.6 132.6 %all-gather.22.cloned.1.call-done = bf16[5632,2048]{1,0:T(8,128)(2,1)} async-done(((bf16[176,2048]{1,0:T(8,128)(2,1)}), bf16[5632,2048]{1,0:T(8,128)(2,1)}) %all-gather.22.cloned.1.call-update) | async-done | bytes 23068688 | tf_op jit(solution)/shard_map/all_gather | solution.py:426
  721.2 14.9 multiply_convert_fusion.2
  736.1 13.1 fusion.226
  749.2 14.0 multiply_reduce_fusion.1
  763.2 12.5 fusion.224
  775.6 12.4 fusion.225
  788.0 15.5 multiply_convert_fusion
  803.5 13.0 fusion.228
  816.5 14.3 multiply_reduce_fusion
  830.8 3.3 multiply_add_fusion.1
  835.2 6.4 convolution_convert_fusion.3
  843.8 53.6 %while.82 = (s32[]{:T(128)}, f32[1,4,8,128,64]{3,4,2,1,0:T(8,128)}, bf16[1,1024,4,64]{1,3,2,0:T(8,128)(2,1)}, bf16[1,1024,4,64]{1,3,2,0:T(8,128)(2,1)}, s32[4]{0...) while((s32[]{:T(128)}, f32[1,4,8,128,64]{3,4,2,1,0:T(8,128)}, ...), condition=%wide.region_23.24_spmd.clone, body=%wide.region_22.23_spmd.clone.sunk | while | flops 682557952 | bytes 66084536 | solution.py:187
  897.5 7.5 convolution_convert_fusion.2
  910.2 54.2 %while.83 = (s32[]{:T(128)}, f32[1,4,8,128,64]{3,4,2,1,0:T(8,128)}, bf16[1,1024,4,64]{1,3,2,0:T(8,128)(2,1)}, bf16[1,1024,4,64]{1,3,2,0:T(8,128)(2,1)}, s32[4]{0...) while((s32[]{:T(128)}, f32[1,4,8,128,64]{3,4,2,1,0:T(8,128)}, ...), condition=%wide.region_30.31_spmd.clone, body=%wide.region_29.30_spmd.clone.sunk | while | flops 682557952 | bytes 66084536 | solution.py:187
  974.2 23.2 reduce-scatter.38.cloned.1.call-done
  1001.7 27.8 reduce-scatter.40.cloned.1.call-done
  1030.6 30.7 reduce-scatter.36.cloned.1.call-done
  1067.9 8.3 convolution_add_fusion.4
  1079.9 8.1 convolution_add_fusion.3
  1089.6 18.1 fusion.230
  1107.8 29.4 convolution_add_fusion.2
  1138.5 17.9 fusion.231
  1156.4 29.4 convolution_add_fusion.1
  1187.4 17.9 fusion.172
  1205.3 29.4 convolution_add_fusion
  1236.0 11.4 fusion.132
  1247.4 11.0 fusion.133
  1269.2 38.0 %all-reduce.4 = (f32[2048]{0:T(1024)S(1)}, f32[2048]{0:T(1024)S(1)}) all-reduce(f32[2048]{0:T(1024)S(1)} %add.420, f32[2048]{0:T(1024)S(1)} %add.424), channel_id=12, replica_groups=mesh['dp'=4,'seq'=8] {'dp','seq'}, use_global_device_ids=true, to_apply=%region_40.41.clone | all-reduce | flops 4096 | bytes 32768
  1311.6 27.1 reduce-scatter.24.cloned.1.call-done
  1338.7 185.5 %reduce-scatter.20.cloned.1.call-done = f32[64,2048]{1,0:T(8,128)} async-done(((f32[2048,2048]{1,0:T(8,128)}), f32[64,2048]{1,0:T(8,128)}) %reduce-scatter.20.cloned.1.call-update) | async-done | bytes 524304 | tf_op jit(solution)/shard_map/reduce_scatter | solution.py:463
  1524.2 187.1 %reduce-scatter.26.cloned.1.call-done = f32[64,2048]{1,0:T(8,128)} async-done(((f32[2048,2048]{1,0:T(8,128)}), f32[64,2048]{1,0:T(8,128)}) %reduce-scatter.26.cloned.1.call-update) | async-done | bytes 524304 | tf_op jit(solution)/shard_map/reduce_scatter | solution.py:466
  1711.3 492.4 %reduce-scatter.28.cloned.1.call-done = f32[64,5632]{1,0:T(8,128)} async-done(((f32[2048,5632]{1,0:T(8,128)}), f32[64,5632]{1,0:T(8,128)}) %reduce-scatter.28.cloned.1.call-update) | async-done | bytes 1441808 | tf_op jit(solution)/shard_map/reduce_scatter | solution.py:468
  2203.7 491.2 %reduce-scatter.30.cloned.1.call-done = f32[64,5632]{1,0:T(8,128)} async-done(((f32[2048,5632]{1,0:T(8,128)}), f32[64,5632]{1,0:T(8,128)}) %reduce-scatter.30.cloned.1.call-update) | async-done | bytes 1441808 | tf_op jit(solution)/shard_map/reduce_scatter | solution.py:469
  2694.9 491.2 %reduce-scatter.32.cloned.1.call-done = f32[176,2048]{1,0:T(8,128)} async-done(((f32[5632,2048]{1,0:T(8,128)}), f32[176,2048]{1,0:T(8,128)}) %reduce-scatter.32.cloned.1.call-update) | async-done | bytes 1441808 | tf_op jit(solution)/shard_map/reduce_scatter | solution.py:470
  (630 shorter events, 233.9 us)
Async XLA Ops:
  7.2 116.3 %copy-start.8 = (bf16[2,128,2048]{2,1,0:T(8,128)(2,1)S(1)}, bf16[2,128,2048]{2,1,0:T(8,128)(2,1)}, u32[]{:S(2)}) copy-start(bf16[2,128,2048]{2,1,0:T(8,128)(2,1)} %param.25) | copy-start | bytes 3145732
  7.2 60.5 %all-gather.10.cloned.1.call-start = ((), (), s32[]{:S(2)}) async-start(), calls=%async_computation.11 | async-start | bytes 1081344 | tf_op jit(solution)/shard_map/all_gather | solution.py:418
  7.9 115.6 %all-gather.14.cloned.1.call-start = ((), (), s32[]{:S(2)}) async-start(), calls=%async_computation.13 | async-start | bytes 1081344 | tf_op jit(solution)/shard_map/all_gather | solution.py:419
  8.7 198.1 %all-gather.12.cloned.1.call-start = ((), (), s32[]{:S(2)}) async-start(), calls=%async_computation.12 | async-start | bytes 8650752 | tf_op jit(solution)/shard_map/all_gather | solution.py:417
  9.4 323.6 %all-gather.16.cloned.1.call-start = ((), (), s32[]{:S(2)}) async-start(), calls=%async_computation.14 | async-start | bytes 8650752 | tf_op jit(solution)/shard_map/all_gather | solution.py:420
  10.0 421.4 %all-gather.18.cloned.1.call-start = ((), (), s32[]{:S(2)}) async-start(), calls=%async_computation.15 | async-start | bytes 23789568 | tf_op jit(solution)/shard_map/all_gather | solution.py:424
  10.6 565.6 %all-gather.20.cloned.1.call-start = ((), (), s32[]{:S(2)}) async-start(), calls=%async_computation.16 | async-start | bytes 23789568 | tf_op jit(solution)/shard_map/all_gather | solution.py:425
  11.1 710.0 %all-gather.22.cloned.1.call-start = ((), (), s32[]{:S(2)}) async-start(), calls=%async_computation.17 | async-start | bytes 23789568 | tf_op jit(solution)/shard_map/all_gather | solution.py:426
  11.9 961.2 %reduce-scatter.34.cloned.1.call-start = ((), (), s32[]{:S(2)}) async-start(), calls=%async_computation.25 | async-start | bytes 589824
  55.9 168.8 %copy-start.63 = (f32[2048]{0:T(1024)}, f32[2048]{0:T(1024)S(1)}, u32[]{:S(2)}) copy-start(f32[2048]{0:T(1024)S(1)} %convert_element_type.350) | copy-start | bytes 24580
  58.4 160.3 %copy-start.83 = (f32[128]{0:T(128)}, f32[128]{0:T(128)S(1)}, u32[]{:S(2)}) copy-start(f32[128]{0:T(128)S(1)} %add_rsqrt_fusion.3) | copy-start | bytes 1540
  58.4 166.3 %copy-start.86 = (f32[128]{0:T(128)}, f32[128]{0:T(128)S(1)}, u32[]{:S(2)}) copy-start(f32[128]{0:T(128)S(1)} %add_rsqrt_fusion.1) | copy-start | bytes 1540
  58.6 168.6 %copy-start.74 = (f32[128,32]{0,1:T(8,128)}, f32[128,32]{0,1:T(8,128)S(1)}, u32[]{:S(2)}) copy-start(f32[128,32]{0,1:T(8,128)S(1)} %get-tuple-element.866) | copy-start | bytes 49156
  58.6 168.6 %copy-start.76 = (f32[128,32]{0,1:T(8,128)}, f32[128,32]{0,1:T(8,128)S(1)}, u32[]{:S(2)}) copy-start(f32[128,32]{0,1:T(8,128)S(1)} %get-tuple-element.867) | copy-start | bytes 49156
  218.7 6.0 copy-start.7
  331.4 6.5 copy-start.29
  332.9 5.1 copy-start.42
  333.0 6.0 copy-start
  333.0 6.3 copy-start.31
  341.7 234.5 %copy-start.23 = (bf16[128,2048]{1,0:T(8,128)(2,1)}, bf16[128,2048]{1,0:T(8,128)(2,1)S(1)}, u32[]{:S(2)}) copy-start(bf16[128,2048]{1,0:T(8,128)(2,1)S(1)} %multiply_convert_fusion.7) | copy-start | bytes 1572868
  443.7 277.5 %copy-start.48 = (bf16[2,128,2048]{2,1,0:T(8,128)(2,1)S(1)}, bf16[2,128,2048]{2,1,0:T(8,128)(2,1)}, u32[]{:S(2)}) copy-start(bf16[2,128,2048]{2,1,0:T(8,128)(2,1)} %param.26) | copy-start | bytes 3145732
  736.1 13.1 copy-start.14
  736.1 13.1 copy-start.16
  763.2 12.5 copy-start.25
  803.5 13.0 copy-start.35
  835.2 6.7 copy-start.50
  835.2 8.6 copy-start.30
  862.7 4.3 copy-start.4
  862.7 4.3 copy-start.60
  876.5 4.3 copy-start.4
  897.5 8.9 copy-start.51
  897.5 9.1 copy-start.59
  905.0 5.2 copy-start.2
  905.0 5.2 copy-start.28
  905.0 5.2 copy-start.79
  905.0 5.2 copy-start.90
  908.4 89.0 %reduce-scatter.38.cloned.1.call-start = ((), (), s32[]{:S(2)}) async-start(), calls=%async_computation.27 | async-start | bytes 589824
  964.4 6.8 copy-start.62
  967.7 61.7 %reduce-scatter.40.cloned.1.call-start = ((), (), s32[]{:S(2)}) async-start(), calls=%async_computation.28 | async-start | bytes 589824
  967.8 30.6 copy-start.75
  967.8 30.6 copy-start.77
  970.2 28.9 copy-start.9
  970.2 28.9 copy-start.64
  970.3 28.9 copy-start.84
  971.2 28.6 copy-start.87
  971.2 90.0 %reduce-scatter.36.cloned.1.call-start = ((), (), s32[]{:S(2)}) async-start(), calls=%async_computation.26 | async-start | bytes 589824
  973.0 338.6 %reduce-scatter.22.cloned.1.call-start = ((), (), s32[]{:S(2)}) async-start(), calls=%async_computation.19 | async-start | bytes 2162688 | tf_op jit(solution)/shard_map/reduce_scatter | solution.py:464
  1001.7 337.1 %reduce-scatter.24.cloned.1.call-start = ((), (), s32[]{:S(2)}) async-start(), calls=%async_computation.20 | async-start | bytes 2162688 | tf_op jit(solution)/shard_map/reduce_scatter | solution.py:465
  1030.5 34.2 %copy-start.68 = (bf16[1,128,256]{1,2,0:T(8,128)(2,1)}, bf16[1,128,256]{1,2,0:T(8,128)(2,1)S(1)}, u32[]{:S(2)}) copy-start(bf16[1,128,256]{1,2,0:T(8,128)(2,1)S(1)} %copy.115) | copy-start | bytes 196612
  1064.7 459.5 %reduce-scatter.20.cloned.1.call-start = ((), (), s32[]{:S(2)}) async-start(), calls=%async_computation.18 | async-start | bytes 17301504 | tf_op jit(solution)/shard_map/reduce_scatter | solution.py:463
  1076.3 635.0 %reduce-scatter.26.cloned.1.call-start = ((), (), s32[]{:S(2)}) async-start(), calls=%async_computation.21 | async-start | bytes 17301504 | tf_op jit(solution)/shard_map/reduce_scatter | solution.py:466
  1088.1 19.6 copy-start.26
  1088.1 1115.6 %reduce-scatter.28.cloned.1.call-start = ((), (), s32[]{:S(2)}) async-start(), calls=%async_computation.22 | async-start | bytes 47579136 | tf_op jit(solution)/shard_map/reduce_scatter | solution.py:468
  1089.6 18.1 copy-start.37
  1137.1 1557.7 %reduce-scatter.30.cloned.1.call-start = ((), (), s32[]{:S(2)}) async-start(), calls=%async_computation.23 | async-start | bytes 47579136 | tf_op jit(solution)/shard_map/reduce_scatter | solution.py:469
  1138.5 17.9 copy-start.36
  1185.8 2000.3 %reduce-scatter.32.cloned.1.call-start = ((), (), s32[]{:S(2)}) async-start(), calls=%async_computation.24 | async-start | bytes 47579136 | tf_op jit(solution)/shard_map/reduce_scatter | solution.py:470
  1187.4 17.9 copy-start.41
  1236.0 11.4 copy-start.15
  1236.0 23.4 slice-start
  1247.4 12.1 slice-start.1
  1247.4 12.0 copy-start.45
  1266.3 42.0 %copy-start.19 = (f32[128,2048]{1,0:T(8,128)S(1)}, f32[128,2048]{1,0:T(8,128)}, u32[]{:S(2)}) copy-start(f32[128,2048]{1,0:T(8,128)} %get-tuple-element.846) | copy-start | bytes 3145732
  1266.3 42.0 %copy-start.22 = (f32[128,2048]{1,0:T(8,128)S(1)}, f32[128,2048]{1,0:T(8,128)}, u32[]{:S(2)}) copy-start(f32[128,2048]{1,0:T(8,128)} %copy-done.20) | copy-start | bytes 3145732
  (83 other events, 203.4 us)
Sparse Core Ops, SparseCore 0:
  11.0 56.6 all-gather.9
  70.7 52.7 all-gather.13
  126.5 80.2 all-gather.11
  209.6 76.5 all-gather.15
  288.9 142.5 all-gather.17
  434.1 142.0 all-gather.19
  579.1 142.0 all-gather.21
  908.5 29.4 reduce-scatter.33
  967.9 29.4 reduce-scatter.37
  1000.0 29.4 reduce-scatter.39
  1031.8 29.4 reduce-scatter.35
  1063.9 136.4 reduce-scatter.21
  1203.2 135.4 reduce-scatter.23
  1341.5 182.6 reduce-scatter.19
  1526.9 184.3 reduce-scatter.25
  1714.0 489.5 reduce-scatter.27
  2206.4 488.4 reduce-scatter.29
  2697.6 488.4 reduce-scatter.31
where the time goes:
time: 3200 us; the launch traced here: 3190 us
  waiting for transfers between devices  2390 us (75%)
  matrix products  492 us (15%)
  blocking collectives  145 us (5%)
  local copies, waits for them, and re-layouts  83.6 us (3%)
  other arithmetic  45.7 us (1%)
    reduce_scatter x1, waiting for transfers between devices, local(): lax.psum_scatter(totals[5], ('dp', 'seq'), scatter_dimension=0, tiled=True)  492 us
    reduce_scatter x1, waiting for transfers between devices, local(): lax.psum_scatter(totals[7], ('dp', 'seq'), scatter_dimension=0, tiled=True)  491 us
    reduce_scatter x1, waiting for transfers between devices, local(): lax.psum_scatter(totals[6], ('dp', 'seq'), scatter_dimension=0, tiled=True)  491 us
    reduce_scatter x1, waiting for transfers between devices, local(): lax.psum_scatter(totals[3], ('dp', 'seq'), scatter_dimension=0, tiled=True)  187 us
    reduce_scatter x1, waiting for transfers between devices, local(): lax.psum_scatter(totals[0], ('dp', 'seq'), scatter_dimension=0, tiled=True)  185 us
    all_gather x1, waiting for transfers between devices, local(): lax.all_gather(w_down, ('dp', 'seq'), axis=0, tiled=True)  133 us
    all_gather x1, waiting for transfers between devices, local(): lax.all_gather(w_up, ('dp', 'seq'), axis=0, tiled=True)  133 us
    all_gather x1, waiting for transfers between devices, local(): lax.all_gather(w_gate, ('dp', 'seq'), axis=0, tiled=True)  89.7 us
  transfers between devices with their start and end apart: 18, of which 15 were waited for; matrix products, arithmetic and copies ran while one was open for 13% of the time, Pallas kernels for 0%

commit v1 on v0

v1 whole, which is shorter than its diff:
```python
import functools
import math

import jax
import jax.numpy as jnp
from jax import lax
from jax.experimental import pallas as pl
from jax.experimental.pallas import tpu as pltpu
from jax.sharding import Mesh, PartitionSpec as P

H = 32
KVH = 4
HD = 64
HALF = HD // 2

epsilon = 1e-05
masked_value = -1e30
rope_base = 10000.0

PLANE = ("dp", "core")
ALL = ("dp", "zz", "core")
f32 = jnp.float32
bf16 = jnp.bfloat16


def rms_scale(values):
    return lax.rsqrt(jnp.mean(values * values, axis=-1, keepdims=True) + epsilon)


def rms_back(grad_normed, values, inverse, gain):
    scaled_grad = grad_normed * gain
    unit_rows = values * inverse
    grad_values = inverse * (
        scaled_grad - unit_rows * jnp.mean(scaled_grad * unit_rows, axis=-1, keepdims=True)
    )
    return (grad_values, jnp.sum(grad_normed * unit_rows, axis=0))


def swap_halves(values):
    width = values.shape[-1]
    lane = lax.broadcasted_iota(jnp.int32, values.shape, 1)
    ahead = pltpu.roll(values, width - HALF, 1)
    behind = pltpu.roll(values, HALF, 1)
    return jnp.where(lane % HD < HALF, -ahead, behind)


def span_bias(scalars, seq_index, pics, seqs, keys, queries):
    key_pos = lax.broadcasted_iota(jnp.int32, (keys, 1), 0)
    query_pos = lax.broadcasted_iota(jnp.int32, (1, queries), 1) + scalars[2 * seqs * pics]
    allowed = key_pos <= query_pos
    for k in range(pics):
        start = scalars[seq_index * pics + k]
        stop = start + scalars[seqs * pics + seq_index * pics + k]
        key_in = (key_pos >= start) & (key_pos < stop)
        query_in = (query_pos >= start) & (query_pos < stop)
        allowed = allowed | (key_in & query_in)
    return jnp.where(allowed, 0.0, masked_value).astype(f32)


def rows_dot(left, right):
    return lax.dot_general(left, right, (((1,), (1,)), ((), ())), preferred_element_type=f32)


def attend_kernel(pics, seqs, heads, scalars, pre_ref, cos_ref, sin_ref, kv_ref, out_ref, q_ref, lse_ref):
    seq_index = pl.program_id(0)
    cores, rows = pre_ref.shape[1], pre_ref.shape[3]
    queries, keys = cores * rows, kv_ref.shape[1]
    width = heads * HD
    pre = pre_ref[0, :, 0, :, :width].reshape(queries, width)
    q = (pre * cos_ref[...] + swap_halves(pre) * sin_ref[...]).astype(bf16) * bf16(0.125)
    q_ref[...] = q.reshape(q_ref.shape)
    kv = kv_ref[0]
    k = kv[:, :HD]
    v_t = kv.T[HD:]
    bias = span_bias(scalars, seq_index, pics, seqs, keys, queries)
    outs = []
    for h in range(heads):
        s = rows_dot(k, q[:, h * HD : (h + 1) * HD]) + bias
        top = jnp.max(s, axis=0, keepdims=True)
        e = jnp.exp(s - top)
        total = jnp.sum(e, axis=0, keepdims=True)
        p = (e * (1.0 / total)).astype(bf16)
        lse_ref[0, h : h + 1, :] = top + jnp.log(total)
        outs.append(jnp.dot(v_t, p, preferred_element_type=f32))
    out = jnp.concatenate(outs, axis=0).T.astype(bf16)
    out_ref[...] = out.reshape(out_ref.shape)


def attend_back_kernel(
    pics, seqs, heads, scalars, q_ref, do_ref, cos_ref, sin_ref, kv_ref, lse_ref, dq_ref, dkv_ref
):
    seq_index = pl.program_id(0)
    cores, rows = q_ref.shape[1], q_ref.shape[3]
    queries, keys = cores * rows, kv_ref.shape[1]
    width = heads * HD
    q = q_ref[...].reshape(queries, width)
    do = do_ref[...].reshape(queries, width)
    kv = kv_ref[0]
    k, v = kv[:, :HD], kv[:, HD:]
    k_t = kv.T[:HD]
    bias = span_bias(scalars, seq_index, pics, seqs, keys, queries)
    dk = jnp.zeros((keys, HD), f32)
    dv = jnp.zeros((keys, HD), f32)
    dqs = []
    for h in range(heads):
        q_h = q[:, h * HD : (h + 1) * HD]
        do_h = do[:, h * HD : (h + 1) * HD]
        p = jnp.exp(rows_dot(k, q_h) + bias - lse_ref[0, h : h + 1, :])
        dp = rows_dot(v, do_h)
        delta = jnp.sum(p * dp, axis=0, keepdims=True)
        ds = (p * (dp - delta)).astype(bf16)
        dv = dv + jnp.dot(p.astype(bf16), do_h, preferred_element_type=f32)
        dk = dk + jnp.dot(ds, q_h, preferred_element_type=f32)
        dqs.append(jnp.dot(k_t, ds, preferred_element_type=f32))
    dq = jnp.concatenate(dqs, axis=0).T * 0.125
    dqp = dq * cos_ref[...] - swap_halves(dq) * sin_ref[...]
    dq_ref[...] = dqp.astype(bf16).reshape(dq_ref.shape)
    dkv_ref[0] = jnp.concatenate([dk, dv], axis=1).astype(bf16)


def plane_gather(values):
    return lax.all_gather(values, PLANE, axis=0, tiled=True)


def plane_reduce(values):
    return lax.psum_scatter(values, PLANE, scatter_dimension=0, tiled=True)


def local(
    tokens,
    cotangent,
    w_query,
    w_key,
    w_value,
    w_output,
    gain_attn,
    w_gate,
    w_up,
    w_down,
    gain_mlp,
    span_start,
    span_len,
):
    nd, nz, nc = lax.axis_size("dp"), lax.axis_size("zz"), lax.axis_size("core")
    plane = nd * nc
    seq_count, row_count, width = tokens.shape
    own = seq_count * row_count
    group = plane * own
    held = w_query.shape[0]
    ff_held = w_down.shape[0]
    heads = H // plane
    q_width = heads * HD
    seqs = nd * seq_count
    pics = span_start.shape[1]
    queries = nc * row_count
    zz, core = lax.axis_index("zz"), lax.axis_index("core")
    whole_heads = held % HD == 0

    def to_inner(values):
        shape = values.shape
        values = values.reshape(shape[:-1] + (nd, nz, nc * held))
        return values.swapaxes(-3, -2).reshape(shape)

    def to_outer(values):
        shape = values.shape
        values = values.reshape(shape[:-1] + (nz, nd, nc * held))
        return values.swapaxes(-3, -2).reshape(shape)

    def by_member(weight, unit):
        weight = weight.reshape(held, nd, nz, nc, unit)
        return weight.transpose(1, 3, 0, 2, 4).reshape(plane, held, nz * unit)

    def from_member(parts, unit):
        parts = parts.reshape(nd, nc, held, nz, unit)
        return parts.transpose(2, 0, 3, 1, 4).reshape(held, nd * nz * nc * unit)

    if whole_heads:
        query_cols = by_member(w_query, held)
    else:
        query_cols = w_query.reshape(held, plane, q_width).transpose(1, 0, 2)
    share = plane // KVH
    key_cols = jnp.repeat(w_key.reshape(held, KVH, HD).transpose(1, 0, 2), share, axis=0)
    value_cols = jnp.repeat(w_value.reshape(held, KVH, HD).transpose(1, 0, 2), share, axis=0)
    columns = jnp.concatenate(
        [query_cols, key_cols, value_cols, by_member(w_gate, ff_held), by_member(w_up, ff_held)],
        axis=-1,
    )
    columns = lax.all_to_all(columns, PLANE, 0, 0, tiled=True)
    qkv_width = q_width + 2 * HD
    ff_width = nz * ff_held

    def z_gather(values):
        return lax.all_gather(values, "zz", axis=0, tiled=True)

    gains = lax.all_gather(jnp.stack([gain_attn, gain_mlp]), ALL, axis=1, tiled=True).astype(f32)
    gain_a, gain_m = gains[0], gains[1]
    spans = lax.all_gather(
        jnp.concatenate([span_start, span_len], axis=1), "dp", axis=0, tiled=True
    )
    scalars = jnp.concatenate(
        [
            spans[:, :pics].reshape(-1),
            spans[:, pics:].reshape(-1),
            (zz * queries).astype(jnp.int32)[None],
        ]
    )

    wqkv = z_gather(columns[:, :, :qkv_width].reshape(plane * held, qkv_width))
    if whole_heads:
        wo = z_gather(w_output)
    else:
        wo = lax.all_gather(w_output, ("zz", "core"), axis=0, tiled=True)
        wo = lax.dynamic_slice_in_dim(wo, core * q_width, q_width, 0)
    wg = z_gather(columns[:, :, qkv_width : qkv_width + ff_width].reshape(plane * held, ff_width))
    wu = z_gather(columns[:, :, qkv_width + ff_width :].reshape(plane * held, ff_width))
    wd = z_gather(w_down)

    positions = (zz * queries + jnp.arange(queries, dtype=jnp.int32)).astype(f32)
    frequency = rope_base ** (-jnp.arange(HALF, dtype=f32) / HALF)
    angles = positions[:, None] * frequency[None, :]
    cosine, sine = jnp.cos(angles), jnp.sin(angles)
    cos_wide = jnp.tile(cosine, (1, q_width // HALF))
    sin_wide = jnp.tile(sine, (1, q_width // HALF))
    cos_k = cosine.reshape(1, nc, 1, row_count, HALF)
    sin_k = sine.reshape(1, nc, 1, row_count, HALF)

    x_low = tokens.reshape(own, width)
    x = x_low.astype(f32)
    inverse_attn = rms_scale(x)
    x_group = plane_gather(x_low).astype(f32)
    normed = to_inner((x_group * rms_scale(x_group) * gain_a).astype(bf16))
    dy_low = cotangent.reshape(own, width)
    dy_group = plane_gather(dy_low)

    pre = jnp.dot(normed, wqkv, preferred_element_type=f32)
    pre = pre.reshape(nd, nc, seq_count, row_count, qkv_width)
    ka, kb = pre[..., q_width : q_width + HALF], pre[..., q_width + HALF : q_width + HD]
    kv = jnp.concatenate(
        [ka * cos_k - kb * sin_k, kb * cos_k + ka * sin_k, pre[..., q_width + HD :]], axis=-1
    ).astype(bf16)
    kv = kv.transpose(0, 2, 1, 3, 4).reshape(seqs, queries, 2 * HD)
    kv_all = lax.all_gather(kv, "zz", axis=1, tiled=True)
    keys = nz * queries

    def token_block(columns_held):
        return pl.BlockSpec(
            (1, nc, 1, row_count, columns_held),
            lambda g, s: (g // seq_count, 0, lax.rem(g, seq_count), 0, 0),
        )

    table_block = pl.BlockSpec((queries, q_width), lambda g, s: (0, 0))
    kv_block = pl.BlockSpec((1, keys, 2 * HD), lambda g, s: (g, 0, 0))
    lse_block = pl.BlockSpec((1, heads, queries), lambda g, s: (g, 0, 0))
    token_shape = jax.ShapeDtypeStruct((nd, nc, seq_count, row_count, q_width), bf16)

    attended, q_kept, lse = pl.pallas_call(
        functools.partial(attend_kernel, pics, seqs, heads),
        out_shape=(
            token_shape,
            token_shape,
            jax.ShapeDtypeStruct((seqs, heads, queries), f32),
        ),
        grid_spec=pltpu.PrefetchScalarGridSpec(
            num_scalar_prefetch=1,
            grid=(seqs,),
            in_specs=[token_block(qkv_width), table_block, table_block, kv_block],
            out_specs=(token_block(q_width), token_block(q_width), lse_block),
        ),
        cost_estimate=pl.CostEstimate(
            flops=4 * seqs * heads * queries * keys * HD,
            bytes_accessed=8 * group * q_width,
            transcendentals=seqs * heads * queries * keys,
        ),
    )(scalars, pre, cos_wide, sin_wide, kv_all)

    attended = attended.reshape(group, q_width)
    mixed = plane_reduce(jnp.dot(attended, wo, preferred_element_type=f32).astype(bf16))
    middle = x + mixed.astype(f32)
    inverse_mlp = rms_scale(middle)
    normed_mid = plane_gather(to_inner((middle * inverse_mlp * gain_m).astype(bf16)))
    gate = jnp.dot(normed_mid, wg, preferred_element_type=f32)
    up = jnp.dot(normed_mid, wu, preferred_element_type=f32)
    sigmoid = jax.nn.sigmoid(gate)
    hidden = (gate * sigmoid * up).astype(bf16)
    grad_hidden = rows_dot(dy_group, wd).astype(bf16).astype(f32)
    grad_gate = (grad_hidden * up * sigmoid * (1.0 + gate * (1.0 - sigmoid))).astype(bf16)
    grad_up = (grad_hidden * gate * sigmoid).astype(bf16)

    back_mid = plane_reduce((rows_dot(grad_gate, wg) + rows_dot(grad_up, wu)).astype(bf16))
    grad_normed_mid = to_outer(back_mid.astype(f32))
    grad_middle_norm, part_gain_mlp = rms_back(grad_normed_mid, middle, inverse_mlp, gain_m)
    grad_middle = dy_low.astype(f32) + grad_middle_norm
    mid_group = plane_gather(grad_middle.astype(bf16))
    grad_mix = rows_dot(mid_group, wo).astype(bf16)

    down = plane_reduce(jnp.dot(hidden, wd, preferred_element_type=f32).astype(bf16))
    layer_out = (middle + down.astype(f32)).astype(bf16).reshape(tokens.shape)

    dq, dkv = pl.pallas_call(
        functools.partial(attend_back_kernel, pics, seqs, heads),
        out_shape=(token_shape, jax.ShapeDtypeStruct((seqs, keys, 2 * HD), bf16)),
        grid_spec=pltpu.PrefetchScalarGridSpec(
            num_scalar_prefetch=1,
            grid=(seqs,),
            in_specs=[
                token_block(q_width),
                token_block(q_width),
                table_block,
                table_block,
                kv_block,
                lse_block,
            ],
            out_specs=(token_block(q_width), kv_block),
        ),
        cost_estimate=pl.CostEstimate(
            flops=10 * seqs * heads * queries * keys * HD,
            bytes_accessed=8 * group * q_width,
            transcendentals=seqs * heads * queries * keys,
        ),
    )(
        scalars,
        q_kept,
        grad_mix.reshape(token_shape.shape),
        cos_wide,
        sin_wide,
        kv_all,
        lse,
    )
    dkv = lax.psum_scatter(dkv, "zz", scatter_dimension=1, tiled=True).astype(f32)
    dkv = dkv.reshape(nd, seq_count, nc, row_count, 2 * HD).transpose(0, 2, 1, 3, 4)
    da, db = dkv[..., :HALF], dkv[..., HALF:HD]
    dkv = jnp.concatenate(
        [da * cos_k + db * sin_k, db * cos_k - da * sin_k, dkv[..., HD:]], axis=-1
    ).astype(bf16)
    dqkv = jnp.concatenate(
        [dq.reshape(group, q_width), dkv.reshape(group, 2 * HD)], axis=-1
    )
    back_in = plane_reduce(rows_dot(dqkv, wqkv).astype(bf16))
    grad_normed = to_outer(back_in.astype(f32))
    grad_input_norm, part_gain_attn = rms_back(grad_normed, x, inverse_attn, gain_a)
    input_grad = (grad_middle + grad_input_norm).astype(bf16).reshape(tokens.shape)

    def columns_dot(left, right):
        return lax.dot_general(
            left, right, (((0,), (0,)), ((), ())), preferred_element_type=f32
        ).astype(bf16)

    def z_reduce(values):
        return lax.psum_scatter(values, "zz", scatter_dimension=0, tiled=True)

    def home(values):
        values = values.reshape(plane, held, values.shape[-1])
        return lax.all_to_all(values, PLANE, 0, 0, tiled=True).astype(f32)

    weight_down = z_reduce(columns_dot(hidden, dy_group)).astype(f32)
    weight_gate = from_member(home(z_reduce(columns_dot(normed_mid, grad_gate))), ff_held)
    weight_up = from_member(home(z_reduce(columns_dot(normed_mid, grad_up))), ff_held)
    weight_output = columns_dot(attended, mid_group)
    if whole_heads:
        weight_output = z_reduce(weight_output).astype(f32)
    else:
        spread = lax.dynamic_update_slice_in_dim(
            jnp.zeros((nc * q_width, width), bf16), weight_output, core * q_width, 0
        )
        weight_output = lax.psum_scatter(
            spread, ("zz", "core"), scatter_dimension=0, tiled=True
        ).astype(f32)
    weight_qkv = home(z_reduce(columns_dot(normed, dqkv)))
    if whole_heads:
        weight_query = from_member(weight_qkv[:, :, :q_width], held)
    else:
        weight_query = weight_qkv[:, :, :q_width].transpose(1, 0, 2).reshape(held, H * HD)

    def kv_home(parts):
        parts = jnp.sum(parts.reshape(KVH, share, held, HD), axis=1)
        return parts.transpose(1, 0, 2).reshape(held, KVH * HD)

    weight_key = kv_home(weight_qkv[:, :, q_width : q_width + HD])
    weight_value = kv_home(weight_qkv[:, :, q_width + HD :])
    gain_grads = lax.psum_scatter(
        jnp.stack([part_gain_attn, part_gain_mlp]), ALL, scatter_dimension=1, tiled=True
    )
    return (
        layer_out,
        input_grad,
        weight_query,
        weight_key,
        weight_value,
        weight_output,
        gain_grads[0],
        weight_gate,
        weight_up,
        weight_down,
        gain_grads[1],
    )


def solution(mesh):
    nd, ns = mesh.shape["dp"], mesh.shape["seq"]
    inner = Mesh(mesh.devices.reshape(nd, ns // 2, 2), ALL)
    rows = P("dp", ("zz", "core"), None)
    weight = P(ALL, None)
    gain = P(ALL)
    spans = P("dp", None)
    return jax.shard_map(
        local,
        mesh=inner,
        in_specs=(rows, rows) + (weight,) * 4 + (gain,) + (weight,) * 3 + (gain, spans, spans),
        out_specs=(rows, rows) + (weight,) * 4 + (gain,) + (weight,) * 3 + (gain,),
        check_vma=False,
    )
```

time: 3200 us -> 1420 us (0.44)
  waiting for transfers between devices: 2390 us -> 917 us
  matrix products: 492 us -> 156 us
  blocking collectives: 145 us -> 50.4 us
  Pallas kernels: 0 us -> 72.6 us
  local copies, waits for them, and re-layouts: 83.6 us -> 138 us
    reduce_scatter x7 -> x10, waiting for transfers between devices: 1870 us -> 401 us  [the longest x4 250 us: plane_reduce(): return lax.psum_scatter(values, PLANE, scatter_dimension=0, tiled=True)]
    dot_general x98 -> x15, matrix products: 492 us -> 156 us  [the longest x5 54.5 us: rows_dot(): lax.dot_general(left, right, (((1,), (1,)), ((), ())), preferred_element_...]
    reshape x0 -> x29, local copies, waits for them, and re-layouts: none -> 90.5 us  [the longest x4 30.4 us: to_inner(): values = values.reshape(shape[:-1] + (nd, nz, nc * held))]
    unnamed x2 -> x0, blocking collectives: 80.1 us -> none
    pallas_call x0 -> x2, Pallas kernels: none -> 72.6 us  [the longest x1 36.3 us: local(): pl.pallas_call(functools.partial(attend_back_kernel, pics, seqs, heads),...]
    all_gather x7 -> x10, waiting for transfers between devices: 430 us -> 369 us  [the longest x4 172 us: plane_gather(): return lax.all_gather(values, PLANE, axis=0, tiled=True)]
    unnamed x22, waiting for transfers between devices: 86.2 us -> 137 us
    all_gather x4 -> x2, blocking collectives: 64.7 us -> 50.4 us  [the longest x1 42.4 us: local(): lax.all_gather(jnp.stack([gain_attn, gain_mlp]), ALL, axis=1, tiled=True)]
  transfers between devices with their start and end apart: 18 -> 25, of which waited for: 15 -> 20; matrix products, arithmetic and copies ran while one was open for 13% -> 18% of each run, Pallas kernels for 0% -> 3%
where the time goes in v1:
time: 1420 us; the launch traced here: 1410 us
  waiting for transfers between devices  917 us (65%)
  matrix products  156 us (11%)
  local copies, waits for them, and re-layouts  138 us (10%)
  Pallas kernels  72.6 us (5%)
  blocking collectives  50.4 us (4%)
  other arithmetic  42.5 us (3%)
  starting transfers between devices  19.8 us (1%)
  between operations  15.1 us (1%)
    reduce_scatter x4, waiting for transfers between devices, plane_reduce(): return lax.psum_scatter(values, PLANE, scatter_dimension=0, tiled=True)  250 us
    all_gather x4, waiting for transfers between devices, plane_gather(): return lax.all_gather(values, PLANE, axis=0, tiled=True)  172 us
    all_gather x5, waiting for transfers between devices, z_gather(): return lax.all_gather(values, 'zz', axis=0, tiled=True)  163 us
    unnamed x22, waiting for transfers between devices  137 us
    reduce_scatter x5, waiting for transfers between devices, z_reduce(): return lax.psum_scatter(values, 'zz', scatter_dimension=0, tiled=True)  130 us
    dot_general x5, matrix products, rows_dot(): lax.dot_general(left, right, (((1,), (1,)), ((), ())), preferred_element_...  54.5 us
    dot_general x5, matrix products, columns_dot(): lax.dot_general(left, right, (((0,), (0,)), ((), ())), preferred_element_...  49.7 us
    all_gather x1, blocking collectives, local(): lax.all_gather(jnp.stack([gain_attn, gain_mlp]), ALL, axis=1, tiled=True)  42.4 us
  transfers between devices with their start and end apart: 25, of which 20 were waited for; matrix products, arithmetic and copies ran while one was open for 18% of the time, Pallas kernels for 3%

profile of v1, /device:TPU:0, one launch (start us, length us, event | category | flops | bytes accessed | tf_op | source)
XLA Modules:
  0.0 1411.1 jit_solution(13603264241207150802)
XLA Ops:
  15.0 4.7 reshape.355
  23.5 5.2 all-to-all-start
  28.8 42.4 %all-gather.1 = bf16[32,64,2]{1,2,0:T(2,128)(2,1)S(1)} all-gather(bf16[1,64,2]{1,2,0:T(2,128)(2,1)S(1)} %maximum_bitcast_fusion.1), channel_id=1, replica_groups=mesh['dp'=4,'zz'=4,'core'=2] {'dp','zz','core'}, dimensions={0}, use_global_device_ids=true | all-gather | bytes 8448 | tf_op jit(solution)/shard_map/all_gather | solution.py:195
  73.0 6.4 all-gather.13.cloned.1.call-done
  79.5 5.1 fusion
  84.6 8.6 fusion.2
  93.2 14.3 %reshape.346 = bf16[2048,4,4,128]{3,2,1,0:T(4,128)(2,1)} reshape(bf16[2048,2048]{1,0:T(8,128)(2,1)} %fusion.2) | data formatting | bytes 16777216 | tf_op jit(solution)/shard_map/reshape | solution.py:161
  107.6 13.8 copy.106
  121.3 14.3 %dot_general.47 = bf16[4,2,2,128,2048]{3,2,1,0,4:T(2,128)(2,1)} reshape(bf16[2048,4,4,128]{0,3,2,1:T(8,128)(2,1)} %bitcast.134) | data formatting | bytes 16777216 | tf_op jit(solution)/shard_map/dot_general | solution.py:235
  135.6 7.5 fusion.3.pre_ref
  146.3 8.0 all-gather
  157.1 33.8 %all-gather.17.cloned.1.call-done.kv_ref = bf16[8,1024,128]{2,1,0:T(8,128)(2,1)} async-done(((bf16[8,256,128]{2,1,0:T(8,128)(2,1)}), bf16[8,1024,128]{2,1,0:T(8,128)(2,1)}) %all-gather.17.cloned.1.call-update) | async-done | bytes 2097168 | tf_op jit(solution)/shard_map/all_gather | solution.py:242
  190.9 36.2 %shard_map.212 = (bf16[4,2,2,128,256]{4,3,2,1,0:T(8,128)(2,1)}, bf16[4,2,2,128,256]{4,3,2,1,0:T(8,128)(2,1)}, f32[8,4,256]{2,1,0:T(4,128)}) custom-call(s32[33]{0:T(128)} %pad_add_fusion.scalars, f32[4,2,2,128,384]{4,3,2,1,0:T(8,128)} %copy-done.3, f32[256,256]{1,0:T(8,128)} %copy.114.cos_ref, f32[256,256]{1,0:T(8,128)} %copy.115.sin_ref, ...), custom_call_target="tpu_custom_call" | custom-call | flops 2147483648 | bytes 4194304 | tf_op jit(solution)/shard_map/pallas_call | solution.py:256
  227.1 7.2 convolution_convert_fusion.2
  237.4 67.4 %reduce-scatter.14.cloned.1.call-done = bf16[256,2048]{1,0:T(8,128)(2,1)} async-done(((bf16[2048,2048]{1,0:T(8,128)(2,1)}), bf16[256,2048]{1,0:T(8,128)(2,1)}) %reduce-scatter.14.cloned.1.call-update) | async-done | bytes 1048592 | tf_op jit(solution)/shard_map/reduce_scatter | solution.py:126
  311.4 54.0 %all-gather.27.cloned.1.call-done = bf16[704,2048]{1,0:T(8,128)(2,1)} async-done(((bf16[176,2048]{1,0:T(8,128)(2,1)}), bf16[704,2048]{1,0:T(8,128)(2,1)}) %all-gather.27.cloned.1.call-update) | async-done | bytes 2883600 | tf_op jit(solution)/shard_map/all_gather | solution.py:193
  365.4 54.9 %all-gather.29.cloned.1.call-done = bf16[2048,2048]{1,0:T(8,128)(2,1)} async-done(((bf16[256,2048]{1,0:T(8,128)(2,1)}), bf16[2048,2048]{1,0:T(8,128)(2,1)}) %all-gather.29.cloned.1.call-update) | async-done | bytes 8388624 | tf_op jit(solution)/shard_map/all_gather | solution.py:122
  420.2 10.6 convolution_convert_fusion.6
  430.8 55.0 %all-gather.23.cloned.1.call-done = bf16[2048,704]{1,0:T(8,128)(2,1)} async-done(((bf16[512,704]{1,0:T(8,128)(2,1)}), bf16[2048,704]{1,0:T(8,128)(2,1)}) %all-gather.23.cloned.1.call-update) | async-done | bytes 2883600 | tf_op jit(solution)/shard_map/all_gather | solution.py:193
  485.8 57.0 %all-gather.21.cloned.1.call-done = bf16[2048,2048]{0,1:T(8,128)(2,1)} async-done(((bf16[256,2048]{0,1:T(8,128)(2,1)}), bf16[2048,2048]{0,1:T(8,128)(2,1)}) %all-gather.21.cloned.1.call-update) | async-done | bytes 8388624 | tf_op jit(solution)/shard_map/all_gather | solution.py:122
  542.9 11.1 fusion.25
  553.9 54.4 %all-gather.25.cloned.1.call-done = bf16[2048,704]{1,0:T(8,128)(2,1)} async-done(((bf16[512,704]{1,0:T(8,128)(2,1)}), bf16[2048,704]{1,0:T(8,128)(2,1)}) %all-gather.25.cloned.1.call-update) | async-done | bytes 2883600 | tf_op jit(solution)/shard_map/all_gather | solution.py:193
  608.3 14.7 %fusion.7 = (bf16[2048,704]{0,1:T(8,128)(2,1)S(1)}, bf16[2048,704]{0,1:T(8,128)(2,1)}) fusion(bf16[2048,704]{0,1:T(8,128)(2,1)} %convolution_convert_fusion.6, f32[2048,704]{0,1:T(8,128)} %fusion.25, bf16[2048,2048]{0,1:T(8,128)(2,1)} %all-gather.21.cloned.1.call-done, bf16[2048,704]{1,0:T(8,128)(2,1)} %all-gather.25.cloned.1.call-done), kind=kOutput, calls=%fused_computation.15 | convolution fusion | flops 5925765120 | bytes 25690112 | tf_op jit(solution)/shard_map/dot_general | solution.py:282
  624.7 10.6 fusion.26
  635.2 16.3 %add_convert_fusion = bf16[2048,2048]{1,0:T(8,128)(2,1)} fusion(f32[2048,2048]{1,0:T(8,128)} %fusion.26, bf16[2048,704]{1,0:T(8,128)(2,1)} %all-gather.25.cloned.1.call-done, f32[2048,704]{0,1:T(8,128)} %fusion.25, bf16[2048,704]{0,1:T(8,128)(2,1)} %convolution_convert_fusion.6), kind=kOutput, calls=%fused_computation.5 | convolution fusion | flops 5924061184 | bytes 36700160 | tf_op jit(solution)/shard_map/dot_general | solution.py:61
  651.6 70.2 %reduce-scatter.18.cloned.1.call-done = bf16[256,2048]{1,0:T(8,128)(2,1)} async-done(((bf16[2048,2048]{1,0:T(8,128)(2,1)}), bf16[256,2048]{1,0:T(8,128)(2,1)}) %reduce-scatter.18.cloned.1.call-update) | async-done | bytes 1048592 | tf_op jit(solution)/shard_map/reduce_scatter | solution.py:126
  721.8 2.8 reshape.403
  733.3 54.0 %all-gather.31.cloned.1.call-done = bf16[2048,2048]{1,0:T(8,128)(2,1)} async-done(((bf16[256,2048]{1,0:T(8,128)(2,1)}), bf16[2048,2048]{1,0:T(8,128)(2,1)}) %all-gather.31.cloned.1.call-update) | async-done | bytes 8388624 | tf_op jit(solution)/shard_map/all_gather | solution.py:122
  787.3 7.0 convolution_convert_fusion.9
  794.2 36.3 %shard_map.213 = (bf16[4,2,2,128,256]{4,3,2,1,0:T(8,128)(2,1)}, bf16[8,1024,128]{2,1,0:T(8,128)(2,1)}) custom-call(s32[33]{0:T(128)} %pad_add_fusion.scalars, bf16[4,2,2,128,256]{4,3,2,1,0:T(8,128)(2,1)} %get-tuple-element.17.q_ref, bf16[4,2,2,128,256]{4,3,2,1,0:T(8,128)(2,1)} %bitcast.191, f32[256,256]{1,0:T(8,128)} %copy.114.cos_ref, ...), custom_call_target="tpu_custom_call" | custom-call | flops 5368709120 | bytes 4194304 | tf_op jit(solution)/shard_map/pallas_call | solution.py:299
  830.6 12.3 convolution_convert_fusion.4
  843.0 10.6 convolution_convert_fusion.5
  853.8 20.5 %reduce-scatter.20.cloned.1.call-done = bf16[8,256,128]{2,1,0:T(8,128)(2,1)} async-done(((bf16[8,1024,128]{2,1,0:T(8,128)(2,1)}), bf16[8,256,128]{2,1,0:T(8,128)(2,1)}) %reduce-scatter.20.cloned.1.call-update) | async-done | bytes 524304 | tf_op jit(solution)/shard_map/reduce_scatter | solution.py:329
  877.3 9.1 convolution_convert_fusion.7
  886.6 10.6 convolution_convert_fusion.3
  897.2 7.0 convolution_convert_fusion.8
  904.6 10.1 convolution_convert_fusion
  914.7 11.4 convolution_convert_fusion.1
  926.1 6.0 reduce-scatter.30.cloned.1.call-done
  934.4 4.2 all-to-all-start.3
  938.6 51.8 %reduce-scatter.28.cloned.1.call-done = bf16[512,704]{0,1:T(8,128)(2,1)} async-done(((bf16[2048,704]{0,1:T(8,128)(2,1)}), bf16[512,704]{0,1:T(8,128)(2,1)}) %reduce-scatter.28.cloned.1.call-update) | async-done | bytes 720912 | tf_op jit(solution)/shard_map/reduce_scatter | solution.py:349
  992.6 4.2 all-to-all-start.2
  996.8 2.8 reshape.393
  999.6 9.8 all-to-all-done.2
  1009.4 18.3 %reduce-scatter.24.cloned.1.call-done = bf16[512,384]{1,0:T(8,128)(2,1)} async-done(((bf16[2048,384]{1,0:T(8,128)(2,1)}), bf16[512,384]{1,0:T(8,128)(2,1)}) %reduce-scatter.24.cloned.1.call-update) | async-done | bytes 393232 | tf_op jit(solution)/shard_map/reduce_scatter | solution.py:349
  1027.7 3.7 all-to-all-start.1
  1032.7 52.4 %reduce-scatter.32.cloned.1.call-done = bf16[176,2048]{1,0:T(8,128)(2,1)} async-done(((bf16[704,2048]{1,0:T(8,128)(2,1)}), bf16[176,2048]{1,0:T(8,128)(2,1)}) %reduce-scatter.32.cloned.1.call-update) | async-done | bytes 720912 | tf_op jit(solution)/shard_map/reduce_scatter | solution.py:349
  1087.4 3.9 reshape.407
  1091.4 4.5 copy.128
  1095.9 4.4 reshape.397
  1100.3 3.9 reshape.405
  1104.2 4.6 copy.126
  1108.7 4.5 reshape.395
  1124.1 2.5 reshape.377
  1126.6 3.1 copy.149
  1129.7 3.2 reshape.378
  1132.9 55.5 %reduce-scatter.22.cloned.1.call-done = bf16[256,2048]{1,0:T(8,128)(2,1)} async-done(((bf16[2048,2048]{1,0:T(8,128)(2,1)}), bf16[256,2048]{1,0:T(8,128)(2,1)}) %reduce-scatter.22.cloned.1.call-update) | async-done | bytes 1048592 | tf_op jit(solution)/shard_map/reduce_scatter | solution.py:126
  1188.3 3.8 reshape.399
  1192.1 3.4 copy.147
  1195.6 3.1 reshape.373
  1198.7 5.8 multiply_reduce_fusion.1
  1205.9 57.2 %reduce-scatter.16.cloned.1.call-done = bf16[256,2048]{1,0:T(8,128)(2,1)} async-done(((bf16[2048,2048]{1,0:T(8,128)(2,1)}), bf16[256,2048]{1,0:T(8,128)(2,1)}) %reduce-scatter.16.cloned.1.call-update) | async-done | bytes 1048592 | tf_op jit(solution)/shard_map/reduce_scatter | solution.py:126
  1263.2 5.5 fusion.14
  1268.7 133.3 %reduce-scatter.34.cloned.1.call-done = f32[64,2]{1,0:T(8,128)} async-done(((f32[2048,2]{1,0:T(8,128)}), f32[64,2]{1,0:T(8,128)}) %reduce-scatter.34.cloned.1.call-update) | async-done | bytes 528
  (164 shorter events, 65.2 us)
Async XLA Ops:
  7.2 4.5 copy-start.4
  7.2 72.3 %all-gather.13.cloned.1.call-start = ((), (), s32[]{:S(2)}) async-start(), calls=%async_computation.15 | async-start | bytes 9437184 | tf_op jit(solution)/shard_map/all_gather | solution.py:122
  21.1 7.6 copy-start.18
  21.2 7.6 copy-start.19
  23.5 47.8 %all-to-all-start = ((bf16[8,64,1792]{2,1,0:T(8,128)(2,1)}), bf16[8,64,1792]{2,1,0:T(8,128)(2,1)S(1)}, u32[]{:S(2)}, u32[]{:S(2)}) async-start(bf16[8,64,1792]{2,1,0:T(8,128)(2,1)} %concatenate.28), calls=%async_computation | async-start | bytes 3670016 | tf_op jit(solution)/shard_map/all_to_all | solution.py:188
  28.7 106.9 %all-gather.15.cloned.1.call-start = ((), (), s32[]{:S(2)}) async-start(), calls=%async_computation.16 | async-start | bytes 1966080 | tf_op jit(solution)/shard_map/all_gather | solution.py:193
  71.3 13.2 copy-start.8
  72.2 118.7 %all-gather.17.cloned.1.call-start = ((), (), s32[]{:S(2)}) async-start(), calls=%async_computation.17 | async-start | bytes 2621440 | tf_op jit(solution)/shard_map/all_gather | solution.py:242
  143.1 1.6 copy-start.3
  143.3 2.9 copy-start.15
  143.3 2.9 copy-start.16
  145.6 81.6 %all-gather.19.cloned.1.call-start = ((), (), s32[]{:S(2)}) async-start(), calls=%async_computation.18 | async-start | bytes 1310720 | tf_op jit(solution)/shard_map/all_gather | solution.py:193
  146.1 158.7 %reduce-scatter.14.cloned.1.call-start = ((), (), s32[]{:S(2)}) async-start(), calls=%async_computation.19 | async-start | bytes 9437184 | tf_op jit(solution)/shard_map/reduce_scatter | solution.py:126
  234.3 70.5 %copy-start = (bf16[2,128,2048]{2,1,0:T(8,128)(2,1)S(1)}, bf16[2,128,2048]{2,1,0:T(8,128)(2,1)}, u32[]{:S(2)}) copy-start(bf16[2,128,2048]{2,1,0:T(8,128)(2,1)} %param.13) | copy-start | bytes 3145732
  234.4 131.0 %all-gather.27.cloned.1.call-start = ((), (), s32[]{:S(2)}) async-start(), calls=%async_computation.23 | async-start | bytes 3604480 | tf_op jit(solution)/shard_map/all_gather | solution.py:193
  234.9 185.3 %all-gather.29.cloned.1.call-start = ((), (), s32[]{:S(2)}) async-start(), calls=%async_computation.25 | async-start | bytes 9437184 | tf_op jit(solution)/shard_map/all_gather | solution.py:122
  235.7 250.2 %all-gather.23.cloned.1.call-start = ((), (), s32[]{:S(2)}) async-start(), calls=%async_computation.21 | async-start | bytes 3932160 | tf_op jit(solution)/shard_map/all_gather | solution.py:193
  237.4 305.5 %all-gather.21.cloned.1.call-start = ((), (), s32[]{:S(2)}) async-start(), calls=%async_computation.20 | async-start | bytes 9437184 | tf_op jit(solution)/shard_map/all_gather | solution.py:122
  306.5 424.3 %copy-start.10 = (f32[256]{0:T(256)}, f32[256]{0:T(256)S(1)}, u32[]{:S(2)}) copy-start(f32[256]{0:T(256)S(1)} %add_rsqrt_fusion.1) | copy-start | bytes 3076
  310.6 297.8 %all-gather.25.cloned.1.call-start = ((), (), s32[]{:S(2)}) async-start(), calls=%async_computation.22 | async-start | bytes 3932160 | tf_op jit(solution)/shard_map/all_gather | solution.py:193
  311.2 410.7 %reduce-scatter.18.cloned.1.call-start = ((), (), s32[]{:S(2)}) async-start(), calls=%async_computation.26 | async-start | bytes 9437184 | tf_op jit(solution)/shard_map/reduce_scatter | solution.py:126
  608.3 16.3 %copy-start.17 = (bf16[2048,704]{1,0:T(8,128)(2,1)S(1)}, bf16[2048,704]{1,0:T(8,128)(2,1)}, u32[]{:S(2)}) copy-start(bf16[2048,704]{1,0:T(8,128)(2,1)} %all-gather.23.cloned.1.call-done) | copy-start | bytes 8650756
  623.0 1.6 copy-start.21
  651.5 135.7 %all-gather.31.cloned.1.call-start = ((), (), s32[]{:S(2)}) async-start(), calls=%async_computation.27 | async-start | bytes 9437184 | tf_op jit(solution)/shard_map/all_gather | solution.py:122
  728.6 2.2 copy-start.1
  728.6 2.2 copy-start.2
  730.8 2.0 copy-start.12
  732.8 141.5 %reduce-scatter.20.cloned.1.call-start = ((), (), s32[]{:S(2)}) async-start(), calls=%async_computation.28 | async-start | bytes 2621440 | tf_op jit(solution)/shard_map/reduce_scatter | solution.py:329
  830.6 101.5 %reduce-scatter.30.cloned.1.call-start = ((), (), s32[]{:S(2)}) async-start(), calls=%async_computation.33 | async-start | bytes 3604480 | tf_op jit(solution)/shard_map/reduce_scatter | solution.py:349
  842.9 147.4 %reduce-scatter.28.cloned.1.call-start = ((), (), s32[]{:S(2)}) async-start(), calls=%async_computation.32 | async-start | bytes 3604480 | tf_op jit(solution)/shard_map/reduce_scatter | solution.py:349
  853.6 174.1 %reduce-scatter.24.cloned.1.call-start = ((), (), s32[]{:S(2)}) async-start(), calls=%async_computation.30 | async-start | bytes 1966080 | tf_op jit(solution)/shard_map/reduce_scatter | solution.py:349
  874.4 3.0 copy-start.20
  875.9 0.8 copy-start.5
  876.4 0.8 copy-start.6
  876.4 1.0 copy-start.7
  886.5 198.6 %reduce-scatter.32.cloned.1.call-start = ((), (), s32[]{:S(2)}) async-start(), calls=%async_computation.34 | async-start | bytes 3604480 | tf_op jit(solution)/shard_map/reduce_scatter | solution.py:349
  897.2 217.7 %reduce-scatter.26.cloned.1.call-start = ((), (), s32[]{:S(2)}) async-start(), calls=%async_computation.31 | async-start | bytes 1310720 | tf_op jit(solution)/shard_map/reduce_scatter | solution.py:349
  904.3 284.0 %reduce-scatter.22.cloned.1.call-start = ((), (), s32[]{:S(2)}) async-start(), calls=%async_computation.29 | async-start | bytes 9437184 | tf_op jit(solution)/shard_map/reduce_scatter | solution.py:126
  914.7 348.5 %reduce-scatter.16.cloned.1.call-start = ((), (), s32[]{:S(2)}) async-start(), calls=%async_computation.24 | async-start | bytes 9437184 | tf_op jit(solution)/shard_map/reduce_scatter | solution.py:126
  934.4 58.3 %all-to-all-start.3 = ((bf16[8,64,704]{2,1,0:T(8,128)(2,1)}), bf16[8,64,704]{2,1,0:T(8,128)(2,1)}, u32[]{:S(2)}, u32[]{:S(2)}) async-start(bf16[8,64,704]{2,1,0:T(8,128)(2,1)} %bitcast.148), calls=%async_computation.12 | async-start | bytes 1572864 | tf_op jit(solution)/shard_map/all_to_all | solution.py:353
  992.6 16.8 %all-to-all-start.2 = ((bf16[8,64,704]{2,1,0:T(8,128)(2,1)}), bf16[8,64,704]{2,1,0:T(8,128)(2,1)}, u32[]{:S(2)}, u32[]{:S(2)}) async-start(bf16[8,64,704]{2,1,0:T(8,128)(2,1)} %bitcast.149), calls=%async_computation.10 | async-start | bytes 1572864 | tf_op jit(solution)/shard_map/all_to_all | solution.py:353
  1027.7 88.9 %all-to-all-start.1 = ((bf16[8,64,384]{2,1,0:T(8,128)(2,1)}), bf16[8,64,384]{2,1,0:T(8,128)(2,1)S(1)}, u32[]{:S(2)}, u32[]{:S(2)}) async-start(bf16[8,64,384]{2,1,0:T(8,128)(2,1)} %bitcast.170), calls=%async_computation.7 | async-start | bytes 786432 | tf_op jit(solution)/shard_map/all_to_all | solution.py:353
  1031.4 370.6 %reduce-scatter.34.cloned.1.call-start = ((), (), s32[]{:S(2)}) async-start(), calls=%async_computation.35 | async-start | bytes 1081344
  1195.6 3.1 copy-start.9
  1195.6 3.1 copy-start.14
  1198.7 64.5 %copy-start.11 = (f32[256]{0:T(256)S(1)}, f32[256]{0:T(256)}, u32[]{:S(2)}) copy-start(f32[256]{0:T(256)} %copy-done.10) | copy-start | bytes 3076
  1198.7 64.5 %copy-start.13 = (f32[256]{0:T(256)S(1)}, f32[256]{0:T(256)}, u32[]{:S(2)}) copy-start(f32[256]{0:T(256)} %copy-done.12) | copy-start | bytes 3076
Sparse Core Ops, SparseCore 0:
  9.9 69.5 all-gather.12
  81.6 36.5 all-gather.14
  145.7 45.1 all-gather.16
  192.3 26.7 all-gather.18
  234.5 70.3 reduce-scatter.13
  306.2 59.0 all-gather.26
  367.3 52.9 all-gather.28
  422.4 63.4 all-gather.22
  488.3 54.5 all-gather.20
  544.8 63.4 all-gather.24
  651.7 70.1 reduce-scatter.17
  733.0 54.2 all-gather.30
  830.7 43.6 reduce-scatter.19
  876.5 55.5 reduce-scatter.29
  934.2 56.0 reduce-scatter.27
  992.5 35.1 reduce-scatter.23
  1029.9 55.1 reduce-scatter.31
  1087.8 27.0 reduce-scatter.25
  1118.3 69.9 reduce-scatter.21
  1191.6 71.4 reduce-scatter.15
  1265.4 136.5 reduce-scatter.33

commit v2 on v1

--- a/solution.py
+++ b/solution.py
@@ -1,5 +1,4 @@
 import functools
-import math
 
 import jax
 import jax.numpy as jnp
@@ -8,6 +7,7 @@
 from jax.experimental.pallas import tpu as pltpu
 from jax.sharding import Mesh, PartitionSpec as P
 
+
 H = 32
 KVH = 4
 HD = 64
@@ -33,7 +33,7 @@
     grad_values = inverse * (
         scaled_grad - unit_rows * jnp.mean(scaled_grad * unit_rows, axis=-1, keepdims=True)
     )
-    return (grad_values, jnp.sum(grad_normed * unit_rows, axis=0))
+    return grad_values
 
 
 def swap_halves(values):
@@ -118,12 +118,274 @@
     dkv_ref[0] = jnp.concatenate([dk, dv], axis=1).astype(bf16)
 
 
-def plane_gather(values):
-    return lax.all_gather(values, PLANE, axis=0, tiled=True)
-
-
-def plane_reduce(values):
-    return lax.psum_scatter(values, PLANE, scatter_dimension=0, tiled=True)
+MESH = pl.DeviceIdType.MESH
+PARTS = 2
+CHUNKS = 2
+
+
+def flip(index, mask):
+    bit = 1
+    while bit <= mask:
+        if mask & bit:
+            index = index + bit - 2 * bit * (index // bit % 2)
+        bit *= 2
+    return index
+
+
+def hops(nd):
+    bits = [1 << i for i in range(nd.bit_length() - 1)]
+    return (bits, bits[::-1])
+
+
+def greet(nd, dp, other):
+    barrier = pltpu.get_barrier_semaphore()
+    bits = hops(nd)[0]
+    for bit in bits:
+        pl.semaphore_signal(
+            barrier, inc=1, device_id={"dp": flip(dp, bit)}, device_id_type=MESH
+        )
+    pl.semaphore_signal(barrier, inc=1, device_id={"core": other}, device_id_type=MESH)
+    pl.semaphore_wait(barrier, len(bits) + 1)
+
+
+def spread_kernel(nd, x_ref, out_ref, held, keep_sem, send, recv, core_send, core_recv):
+    dp, core = lax.axis_index("dp"), lax.axis_index("core")
+    other = 1 - core
+    rows = x_ref.shape[0] // (PARTS * CHUNKS)
+    greet(nd, dp, other)
+    orders = hops(nd)
+    pieces = [(c, p) for c in range(CHUNKS) for p in range(PARTS)]
+
+    def span(c, p):
+        return pl.ds((p * CHUNKS + c) * rows, rows)
+
+    def hop(c, p, mask, bit):
+        place = out_ref.at[flip(dp, mask), core, span(c, p)]
+        source = x_ref.at[span(c, p)] if mask == 0 else place
+        index = (p * CHUNKS + c) * nd + mask + bit
+        return pltpu.make_async_remote_copy(
+            src_ref=source,
+            dst_ref=place,
+            send_sem=send.at[index],
+            recv_sem=recv.at[index],
+            device_id={"dp": flip(dp, bit)},
+            device_id_type=MESH,
+        )
+
+    def share(c, p, mask):
+        place = out_ref.at[flip(dp, mask), core, span(c, p)]
+        source = x_ref.at[span(c, p)] if mask == 0 else place
+        index = (p * CHUNKS + c) * nd + mask
+        return pltpu.make_async_remote_copy(
+            src_ref=source,
+            dst_ref=place,
+            send_sem=core_send.at[index],
+            recv_sem=core_recv.at[index],
+            device_id={"core": other},
+            device_id_type=MESH,
+        )
+
+    started = []
+    for position in range(len(orders[0])):
+        for c, p in pieces:
+            copy = hop(c, p, 0, orders[p][position])
+            copy.start()
+            started.append(copy)
+    for c, p in pieces:
+        copy = share(c, p, 0)
+        copy.start()
+        started.append(copy)
+    load = pltpu.make_async_copy(x_ref, held, keep_sem.at[0])
+    load.start()
+    load.wait()
+    store = pltpu.make_async_copy(held, out_ref.at[dp, core], keep_sem.at[1])
+    store.start()
+    for size in range(1, len(orders[0]) + 1):
+        for c, p in pieces:
+            order = orders[p]
+            for mask in range(1, nd):
+                if bin(mask).count("1") != size:
+                    continue
+                last = max(i for i, bit in enumerate(order) if mask & bit)
+                hop(c, p, mask - order[last], order[last]).wait_recv()
+                for bit in order[last + 1 :]:
+                    copy = hop(c, p, mask, bit)
+                    copy.start()
+                    started.append(copy)
+                copy = share(c, p, mask)
+                copy.start()
+                started.append(copy)
+    for c, p in pieces:
+        for mask in range(nd):
+            share(c, p, mask).wait_recv()
+    for copy in started:
+        copy.wait_send()
+    store.wait()
+
+
+def collect_kernel(
+    nd, order_out, x_ref, out_ref, mine, from_core, out_box, in_box, load_sem, send, recv, core_send, core_recv
+):
+    dp, core = lax.axis_index("dp"), lax.axis_index("core")
+    other = 1 - core
+    rows = out_ref.shape[0] // (PARTS * CHUNKS)
+    greet(nd, dp, other)
+    orders = hops(nd)
+
+    def span(c, p):
+        return pl.ds((p * CHUNKS + c) * rows, rows)
+
+    def share(c, p, mask):
+        index = (p * CHUNKS + c) * nd + mask
+        return pltpu.make_async_remote_copy(
+            src_ref=x_ref.at[flip(dp, mask), other, span(c, p)],
+            dst_ref=from_core.at[mask, span(c, p)],
+            send_sem=core_send.at[index],
+            recv_sem=core_recv.at[index],
+            device_id={"core": other},
+            device_id_type=MESH,
+        )
+
+    def hop(c, p, mask):
+        index = (p * CHUNKS + c) * nd + mask
+        bit = next(bit for bit in orders[p] if mask & bit)
+        return pltpu.make_async_remote_copy(
+            src_ref=out_box.at[mask, span(c, p)],
+            dst_ref=in_box.at[mask, span(c, p)],
+            send_sem=send.at[index],
+            recv_sem=recv.at[index],
+            device_id={"dp": flip(dp, bit)},
+            device_id_type=MESH,
+        )
+
+    def stage(p, mask):
+        order = orders[p]
+        return next((i for i, bit in enumerate(order) if mask & bit), len(order))
+
+    steps = []
+    for position in range(len(orders[0]) + 1):
+        for c in range(CHUNKS):
+            for p in range(PARTS):
+                masks = [m for m in range(nd - 1, -1, -1) if stage(p, m) == position]
+                steps += [(c, p, m) for m in masks]
+    started = []
+    for c, p, mask in steps:
+        copy = share(c, p, mask)
+        copy.start()
+        started.append(copy)
+    loads = [
+        pltpu.make_async_copy(x_ref.at[flip(dp, mask), core], mine.at[mask], load_sem.at[mask])
+        for mask in range(nd)
+    ]
+    for load in loads:
+        load.start()
+    for load in loads:
+        load.wait()
+    step_rows = 16
+    for c, p, mask in steps:
+        order = orders[p]
+        arrived = [mask + bit for bit in order[: stage(p, mask)]]
+        share(c, p, mask).wait_recv()
+        for m in arrived:
+            hop(c, p, m).wait_recv()
+        first = (p * CHUNKS + c) * rows
+
+        def add(i, carry, mask=mask, arrived=arrived, first=first):
+            at = pl.ds(pl.multiple_of(first + i * step_rows, step_rows), step_rows)
+            total = mine[mask, at].astype(f32) + from_core[mask, at].astype(f32)
+            for m in arrived:
+                total = total + in_box[m, at].astype(f32)
+            if mask == 0:
+                block = total.shape[1] // len(order_out)
+                for place, source in enumerate(order_out):
+                    out_ref[at, place * block : (place + 1) * block] = total[
+                        :, source * block : (source + 1) * block
+                    ]
+            else:
+                out_box[mask, at] = total.astype(bf16)
+            return carry
+
+        lax.fori_loop(0, rows // step_rows, add, 0)
+        if mask:
+            copy = hop(c, p, mask)
+            copy.start()
+            started.append(copy)
+    for copy in started:
+        copy.wait_send()
+
+
+def place_kernel(nd, nz, nc, unit, parts_ref, out_ref):
+    for d in range(nd):
+        for c in range(nc):
+            part = parts_ref[d * nc + c].astype(f32)
+            for z in range(nz):
+                at = ((d * nz + z) * nc + c) * unit
+                out_ref[:, at : at + unit] = part[:, z * unit : (z + 1) * unit]
+
+
+def place_columns(parts, nd, nz, nc, unit):
+    held = parts.shape[1]
+    return pl.pallas_call(
+        functools.partial(place_kernel, nd, nz, nc, unit),
+        out_shape=jax.ShapeDtypeStruct((held, nd * nz * nc * unit), f32),
+        in_specs=[pl.BlockSpec(memory_space=pltpu.VMEM)],
+        out_specs=pl.BlockSpec(memory_space=pltpu.VMEM),
+        cost_estimate=pl.CostEstimate(
+            flops=0, bytes_accessed=6 * parts.size, transcendentals=0
+        ),
+    )(parts)
+
+
+def plane_gather(values, nd, nc, ident):
+    rows, width = values.shape
+    sems = PARTS * CHUNKS * nd
+    out = pl.pallas_call(
+        functools.partial(spread_kernel, nd),
+        out_shape=jax.ShapeDtypeStruct((nd, nc, rows, width), values.dtype),
+        in_specs=[pl.BlockSpec(memory_space=pl.ANY)],
+        out_specs=pl.BlockSpec(memory_space=pl.ANY),
+        scratch_shapes=[
+            pltpu.VMEM((rows, width), values.dtype),
+            pltpu.SemaphoreType.DMA((2,)),
+            pltpu.SemaphoreType.DMA((sems,)),
+            pltpu.SemaphoreType.DMA((sems,)),
+            pltpu.SemaphoreType.DMA((sems,)),
+            pltpu.SemaphoreType.DMA((sems,)),
+        ],
+        compiler_params=pltpu.CompilerParams(collective_id=ident, has_side_effects=True),
+        cost_estimate=pl.CostEstimate(
+            flops=0, bytes_accessed=16 * nd * rows * width, transcendentals=0
+        ),
+    )(values)
+    return out.reshape(nd * nc * rows, width)
+
+
+def plane_reduce(values, nd, nc, ident, order=(0,)):
+    width = values.shape[1]
+    rows = values.shape[0] // (nd * nc)
+    sems = PARTS * CHUNKS * nd
+    box = pltpu.VMEM((nd, rows, width), bf16)
+    return pl.pallas_call(
+        functools.partial(collect_kernel, nd, tuple(order)),
+        out_shape=jax.ShapeDtypeStruct((rows, width), f32),
+        in_specs=[pl.BlockSpec(memory_space=pl.ANY)],
+        out_specs=pl.BlockSpec(memory_space=pltpu.VMEM),
+        scratch_shapes=[
+            box,
+            box,
+            box,
+            box,
+            pltpu.SemaphoreType.DMA((nd,)),
+            pltpu.SemaphoreType.DMA((sems,)),
+            pltpu.SemaphoreType.DMA((sems,)),
+            pltpu.SemaphoreType.DMA((sems,)),
+            pltpu.SemaphoreType.DMA((sems,)),
+        ],
+        compiler_params=pltpu.CompilerParams(collective_id=ident, has_side_effects=True),
+        cost_estimate=pl.CostEstimate(
+            flops=0, bytes_accessed=16 * nd * rows * width, transcendentals=0
+        ),
+    )(values.reshape(nd, nc, rows, width))
 
 
 def local(
@@ -156,15 +418,29 @@
     zz, core = lax.axis_index("zz"), lax.axis_index("core")
     whole_heads = held % HD == 0
 
-    def to_inner(values):
-        shape = values.shape
-        values = values.reshape(shape[:-1] + (nd, nz, nc * held))
-        return values.swapaxes(-3, -2).reshape(shape)
-
-    def to_outer(values):
-        shape = values.shape
-        values = values.reshape(shape[:-1] + (nz, nd, nc * held))
-        return values.swapaxes(-3, -2).reshape(shape)
+    def gather(values, ident):
+        return plane_gather(values, nd, nc, ident)
+
+    def reduce(values, ident):
+        return plane_reduce(values, nd, nc, ident)
+
+    feature_block = nc * held
+
+    def to_weight_order(values):
+        values = values.reshape(own, nd, nz, feature_block)
+        return values.swapaxes(1, 2).reshape(own, width)
+
+    def to_feature_order(values):
+        values = values.reshape(own, nz, nd, feature_block)
+        return values.swapaxes(1, 2).reshape(own, width)
+
+    def reduce_features(values, ident):
+        if feature_block % 128:
+            return to_feature_order(reduce(values, ident))
+        order = [z * nd + d for d in range(nd) for z in range(nz)]
+        return plane_reduce(values, nd, nc, ident, order)
+
+    tie = lax.optimization_barrier
 
     def by_member(weight, unit):
         weight = weight.reshape(held, nd, nz, nc, unit)
@@ -181,39 +457,52 @@
     share = plane // KVH
     key_cols = jnp.repeat(w_key.reshape(held, KVH, HD).transpose(1, 0, 2), share, axis=0)
     value_cols = jnp.repeat(w_value.reshape(held, KVH, HD).transpose(1, 0, 2), share, axis=0)
-    columns = jnp.concatenate(
-        [query_cols, key_cols, value_cols, by_member(w_gate, ff_held), by_member(w_up, ff_held)],
-        axis=-1,
-    )
-    columns = lax.all_to_all(columns, PLANE, 0, 0, tiled=True)
     qkv_width = q_width + 2 * HD
     ff_width = nz * ff_held
 
+    def to_members(columns):
+        return lax.all_to_all(columns, PLANE, 0, 0, tiled=True)
+
     def z_gather(values):
         return lax.all_gather(values, "zz", axis=0, tiled=True)
 
-    gains = lax.all_gather(jnp.stack([gain_attn, gain_mlp]), ALL, axis=1, tiled=True).astype(f32)
-    gain_a, gain_m = gains[0], gains[1]
-    spans = lax.all_gather(
-        jnp.concatenate([span_start, span_len], axis=1), "dp", axis=0, tiled=True
-    )
+    spans = jnp.concatenate([span_start.reshape(-1), span_len.reshape(-1)])
+    small = jnp.concatenate(
+        [gain_attn, gain_mlp, (spans // 32).astype(bf16), (spans % 32).astype(bf16)]
+    )
+    small = jnp.pad(small, (0, qkv_width - small.shape[0]))
+    small = jnp.broadcast_to(small, (plane, 1, qkv_width))
+    small = jnp.pad(small, ((0, 0), (0, 15), (0, 0)))
+    columns = jnp.concatenate(
+        [jnp.concatenate([query_cols, key_cols, value_cols], axis=-1), small], axis=1
+    )
+    columns = z_gather(to_members(columns)).reshape(nz, nd, nc, held + 16, qkv_width)
+    wqkv = columns[:, :, :, :held].reshape(width, qkv_width)
+    small = columns[:, :, :, held]
+    gains = small[..., : 2 * held].astype(f32)
+    gain_a_weight_order = gains[..., :held].reshape(width)
+    gains = gains.transpose(1, 0, 2, 3)
+    gain_a = gains[..., :held].reshape(width)
+    gain_m = gains[..., held:].reshape(width)
+    split = seq_count * pics
+    spans = small[0, :, 0, 2 * held : 2 * held + 4 * split].astype(jnp.int32)
+    spans = spans[:, : 2 * split] * 32 + spans[:, 2 * split :]
     scalars = jnp.concatenate(
         [
-            spans[:, :pics].reshape(-1),
-            spans[:, pics:].reshape(-1),
+            spans[:, :split].reshape(-1),
+            spans[:, split:].reshape(-1),
             (zz * queries).astype(jnp.int32)[None],
         ]
     )
 
-    wqkv = z_gather(columns[:, :, :qkv_width].reshape(plane * held, qkv_width))
     if whole_heads:
         wo = z_gather(w_output)
     else:
         wo = lax.all_gather(w_output, ("zz", "core"), axis=0, tiled=True)
         wo = lax.dynamic_slice_in_dim(wo, core * q_width, q_width, 0)
-    wg = z_gather(columns[:, :, qkv_width : qkv_width + ff_width].reshape(plane * held, ff_width))
-    wu = z_gather(columns[:, :, qkv_width + ff_width :].reshape(plane * held, ff_width))
-    wd = z_gather(w_down)
+    ff_columns = to_members(
+        jnp.concatenate([by_member(w_gate, ff_held), by_member(w_up, ff_held)], axis=-1)
+    )
 
     positions = (zz * queries + jnp.arange(queries, dtype=jnp.int32)).astype(f32)
     frequency = rope_base ** (-jnp.arange(HALF, dtype=f32) / HALF)
@@ -227,10 +516,9 @@
     x_low = tokens.reshape(own, width)
     x = x_low.astype(f32)
     inverse_attn = rms_scale(x)
-    x_group = plane_gather(x_low).astype(f32)
-    normed = to_inner((x_group * rms_scale(x_group) * gain_a).astype(bf16))
+    x_group = gather(to_weight_order(x_low), 1).astype(f32)
+    normed = (x_group * rms_scale(x_group) * gain_a_weight_order).astype(bf16)
     dy_low = cotangent.reshape(own, width)
-    dy_group = plane_gather(dy_low)
 
     pre = jnp.dot(normed, wqkv, preferred_element_type=f32)
     pre = pre.reshape(nd, nc, seq_count, row_count, qkv_width)
@@ -239,7 +527,13 @@
         [ka * cos_k - kb * sin_k, kb * cos_k + ka * sin_k, pre[..., q_width + HD :]], axis=-1
     ).astype(bf16)
     kv = kv.transpose(0, 2, 1, 3, 4).reshape(seqs, queries, 2 * HD)
+    kv, wo, dy_late = tie((kv, wo, dy_low))
     kv_all = lax.all_gather(kv, "zz", axis=1, tiled=True)
+    dy_group = gather(dy_late, 2)
+    kv_all, dy_group, ff_columns, down_rows = tie((kv_all, dy_group, ff_columns, w_down))
+    wg = z_gather(ff_columns[:, :, :ff_width].reshape(plane * held, ff_width))
+    wu = z_gather(ff_columns[:, :, ff_width:].reshape(plane * held, ff_width))
+    wd = z_gather(down_rows)
     keys = nz * queries
 
     def token_block(columns_held):
@@ -274,27 +568,48 @@
     )(scalars, pre, cos_wide, sin_wide, kv_all)
 
     attended = attended.reshape(group, q_width)
-    mixed = plane_reduce(jnp.dot(attended, wo, preferred_element_type=f32).astype(bf16))
-    middle = x + mixed.astype(f32)
+    mixed = reduce(jnp.dot(attended, wo, preferred_element_type=f32).astype(bf16), 5)
+    middle = x + mixed
     inverse_mlp = rms_scale(middle)
-    normed_mid = plane_gather(to_inner((middle * inverse_mlp * gain_m).astype(bf16)))
+    normed_mid = gather(
+        to_weight_order((middle * inverse_mlp * gain_m).astype(bf16)), 3
+    )
     gate = jnp.dot(normed_mid, wg, preferred_element_type=f32)
     up = jnp.dot(normed_mid, wu, preferred_element_type=f32)
     sigmoid = jax.nn.sigmoid(gate)
     hidden = (gate * sigmoid * up).astype(bf16)
-    grad_hidden = rows_dot(dy_group, wd).astype(bf16).astype(f32)
+
+    def columns_dot(left, right):
+        return lax.dot_general(
+            left, right, (((0,), (0,)), ((), ())), preferred_element_type=f32
+        ).astype(bf16)
+
+    def z_reduce(values):
+        return lax.psum_scatter(values, "zz", scatter_dimension=0, tiled=True)
+
+    def home(values):
+        values = values.reshape(plane, held, values.shape[-1])
+        return lax.all_to_all(values, PLANE, 0, 0, tiled=True)
+
+    dy_late, weight_down = tie((dy_group, columns_dot(hidden, dy_group)))
+    weight_down = z_reduce(weight_down).astype(f32)
+    grad_hidden = rows_dot(dy_late, wd).astype(bf16).astype(f32)
     grad_gate = (grad_hidden * up * sigmoid * (1.0 + gate * (1.0 - sigmoid))).astype(bf16)
     grad_up = (grad_hidden * gate * sigmoid).astype(bf16)
-
-    back_mid = plane_reduce((rows_dot(grad_gate, wg) + rows_dot(grad_up, wu)).astype(bf16))
-    grad_normed_mid = to_outer(back_mid.astype(f32))
-    grad_middle_norm, part_gain_mlp = rms_back(grad_normed_mid, middle, inverse_mlp, gain_m)
+    weight_gate = columns_dot(normed_mid, grad_gate)
+    weight_up = columns_dot(normed_mid, grad_up)
+    back_mid = (rows_dot(grad_gate, wg) + rows_dot(grad_up, wu)).astype(bf16)
+    back_mid, weight_gate, weight_up = tie((back_mid, weight_gate, weight_up))
+    weight_gate = z_reduce(weight_gate)
+    weight_up = z_reduce(weight_up)
+    weight_gate = place_columns(home(weight_gate), nd, nz, nc, ff_held)
+    weight_up = place_columns(home(weight_up), nd, nz, nc, ff_held)
+
+    grad_normed_mid = reduce_features(back_mid, 6)
+    grad_middle_norm = rms_back(grad_normed_mid, middle, inverse_mlp, gain_m)
     grad_middle = dy_low.astype(f32) + grad_middle_norm
-    mid_group = plane_gather(grad_middle.astype(bf16))
+    mid_group = gather(grad_middle.astype(bf16), 4)
     grad_mix = rows_dot(mid_group, wo).astype(bf16)
-
-    down = plane_reduce(jnp.dot(hidden, wd, preferred_element_type=f32).astype(bf16))
-    layer_out = (middle + down.astype(f32)).astype(bf16).reshape(tokens.shape)
 
     dq, dkv = pl.pallas_call(
         functools.partial(attend_back_kernel, pics, seqs, heads),
@@ -326,7 +641,13 @@
         kv_all,
         lse,
     )
-    dkv = lax.psum_scatter(dkv, "zz", scatter_dimension=1, tiled=True).astype(f32)
+    down = jnp.dot(hidden, wd, preferred_element_type=f32).astype(bf16)
+    down, dq, dkv = tie((down, dq, dkv))
+    dkv = lax.psum_scatter(dkv, "zz", scatter_dimension=1, tiled=True)
+    down = reduce(down, 7)
+    down, dkv, attended_late = tie((down, dkv, attended))
+    layer_out = (middle + down).astype(bf16).reshape(tokens.shape)
+    dkv = dkv.astype(f32)
     dkv = dkv.reshape(nd, seq_count, nc, row_count, 2 * HD).transpose(0, 2, 1, 3, 4)
     da, db = dkv[..., :HALF], dkv[..., HALF:HD]
     dkv = jnp.concatenate(
@@ -335,27 +656,11 @@
     dqkv = jnp.concatenate(
         [dq.reshape(group, q_width), dkv.reshape(group, 2 * HD)], axis=-1
     )
-    back_in = plane_reduce(rows_dot(dqkv, wqkv).astype(bf16))
-    grad_normed = to_outer(back_in.astype(f32))
-    grad_input_norm, part_gain_attn = rms_back(grad_normed, x, inverse_attn, gain_a)
-    input_grad = (grad_middle + grad_input_norm).astype(bf16).reshape(tokens.shape)
-
-    def columns_dot(left, right):
-        return lax.dot_general(
-            left, right, (((0,), (0,)), ((), ())), preferred_element_type=f32
-        ).astype(bf16)
-
-    def z_reduce(values):
-        return lax.psum_scatter(values, "zz", scatter_dimension=0, tiled=True)
-
-    def home(values):
-        values = values.reshape(plane, held, values.shape[-1])
-        return lax.all_to_all(values, PLANE, 0, 0, tiled=True).astype(f32)
-
-    weight_down = z_reduce(columns_dot(hidden, dy_group)).astype(f32)
-    weight_gate = from_member(home(z_reduce(columns_dot(normed_mid, grad_gate))), ff_held)
-    weight_up = from_member(home(z_reduce(columns_dot(normed_mid, grad_up))), ff_held)
-    weight_output = columns_dot(attended, mid_group)
+    weight_qkv = columns_dot(normed, dqkv)
+    back_in, weight_qkv = tie((rows_dot(dqkv, wqkv).astype(bf16), weight_qkv))
+    weight_qkv = z_reduce(weight_qkv)
+    weight_qkv = home(weight_qkv).astype(f32)
+    weight_output = columns_dot(attended_late, mid_group)
     if whole_heads:
         weight_output = z_reduce(weight_output).astype(f32)
     else:
@@ -365,7 +670,10 @@
         weight_output = lax.psum_scatter(
             spread, ("zz", "core"), scatter_dimension=0, tiled=True
         ).astype(f32)
-    weight_qkv = home(z_reduce(columns_dot(normed, dqkv)))
+    grad_normed = reduce_features(back_in, 8)
+    grad_input_norm = rms_back(grad_normed, x, inverse_attn, gain_a)
+    input_grad = (grad_middle + grad_input_norm).astype(bf16).reshape(tokens.shape)
+
     if whole_heads:
         weight_query = from_member(weight_qkv[:, :, :q_width], held)
     else:
@@ -377,9 +685,15 @@
 
     weight_key = kv_home(weight_qkv[:, :, q_width : q_width + HD])
     weight_value = kv_home(weight_qkv[:, :, q_width + HD :])
-    gain_grads = lax.psum_scatter(
-        jnp.stack([part_gain_attn, part_gain_mlp]), ALL, scatter_dimension=1, tiled=True
-    )
+
+    def gain_grad(pairs, gain):
+        terms = (jnp.sum(w.astype(f32) * grad, axis=1) for w, grad in pairs)
+        return sum(terms) / gain.astype(f32)
+
+    grad_gain_attn = gain_grad(
+        ((w_query, weight_query), (w_key, weight_key), (w_value, weight_value)), gain_attn
+    )
+    grad_gain_mlp = gain_grad(((w_gate, weight_gate), (w_up, weight_up)), gain_mlp)
     return (
         layer_out,
         input_grad,
@@ -387,11 +701,11 @@
         weight_key,
         weight_value,
         weight_output,
-        gain_grads[0],
+        grad_gain_attn,
         weight_gate,
         weight_up,
         weight_down,
-        gain_grads[1],
+        grad_gain_mlp,
     )
 
 

time: 1420 us -> 891 us (0.63)
  waiting for transfers between devices: 917 us -> 159 us
  Pallas kernels: 72.6 us -> 423 us
  local copies, waits for them, and re-layouts: 138 us -> 45.3 us
  blocking collectives: 50.4 us -> 14.5 us
    pallas_call x0 -> x10, Pallas kernels: none -> 349 us  [the longest x4 173 us: plane_reduce(): pl.pallas_call(functools.partial(collect_kernel, nd, tuple(order)), out_s...]
    reduce_scatter x5 -> x1, waiting for transfers between devices: 271 us -> 0.02 us  [local(): dkv = lax.psum_scatter(dkv, 'zz', scatter_dimension=1, tiled=True)]
    all_gather x4 -> x0, waiting for transfers between devices: 172 us -> none  [plane_gather(): return lax.all_gather(values, PLANE, axis=0, tiled=True)]
    all_gather x5, waiting for transfers between devices: 163 us -> 22.4 us  [z_gather(): return lax.all_gather(values, 'zz', axis=0, tiled=True)]
    unnamed x22 -> x12, waiting for transfers between devices: 137 us -> 3.26 us
    all_gather x2 -> x0, blocking collectives: 50.4 us -> none  [the longest x1 42.4 us: local(): lax.all_gather(jnp.stack([gain_attn, gain_mlp]), ALL, axis=1, tiled=True)]
    all_gather x1, waiting for transfers between devices: 33.8 us -> 0.02 us  [local(): kv_all = lax.all_gather(kv, 'zz', axis=1, tiled=True)]
    reshape x10 -> x7, local copies, waits for them, and re-layouts: 40.4 us -> 8.47 us  [the longest x2 4.22 us: to_weight_order(): return values.swapaxes(1, 2).reshape(own, width)]
  transfers between devices with their start and end apart: 25 -> 16, of which waited for: 20 -> 8; matrix products, arithmetic and copies ran while one was open for 18% -> 17% of each run, Pallas kernels for 3% -> 35%
where the time goes in v2:
time: 891 us; the launch traced here: 883 us
  Pallas kernels  423 us (47%)
  waiting for transfers between devices  159 us (18%)
  matrix products  154 us (17%)
  other arithmetic  54.7 us (6%)
  local copies, waits for them, and re-layouts  45.3 us (5%)
  starting transfers between devices  16.5 us (2%)
  between operations  15.5 us (2%)
  blocking collectives  14.5 us (2%)
    pallas_call x4, Pallas kernels, plane_reduce(): pl.pallas_call(functools.partial(collect_kernel, nd, tuple(order)), out_s...  173 us
    pallas_call x4, Pallas kernels, plane_gather(): pl.pallas_call(functools.partial(spread_kernel, nd), out_shape=jax.ShapeD...  171 us
    reduce_scatter x5, waiting for transfers between devices, z_reduce(): return lax.psum_scatter(values, 'zz', scatter_dimension=0, tiled=True)  127 us
    dot_general x5, matrix products, rows_dot(): lax.dot_general(left, right, (((1,), (1,)), ((), ())), preferred_element_...  57.8 us
    dot_general x5, matrix products, columns_dot(): lax.dot_general(left, right, (((0,), (0,)), ((), ())), preferred_element_...  46.7 us
    pallas_call x1, Pallas kernels, local(): pl.pallas_call(functools.partial(attend_kernel, pics, seqs, heads), out_s...  36.9 us
    pallas_call x1, Pallas kernels, local(): pl.pallas_call(functools.partial(attend_back_kernel, pics, seqs, heads),...  36.5 us
    all_gather x5, waiting for transfers between devices, z_gather(): return lax.all_gather(values, 'zz', axis=0, tiled=True)  22.4 us
  transfers between devices with their start and end apart: 16, of which 8 were waited for; matrix products, arithmetic and copies ran while one was open for 17% of the time, Pallas kernels for 35%

profile of v2, /device:TPU:0, one launch (start us, length us, event | category | flops | bytes accessed | tf_op | source)
XLA Modules:
  0.0 882.6 jit_solution(4952951533672110430)
XLA Ops:
  12.1 14.5 %all_to_all.25 = bf16[8,80,384]{2,1,0:T(8,128)(2,1)} all-to-all(bf16[8,80,384]{2,1,0:T(8,128)(2,1)S(1)} %fusion.16), channel_id=1, replica_groups=mesh['dp'=4,'zz'=4,'core'=2] {'dp','core'}, dimensions={0} | all-to-all | bytes 983040 | tf_op jit(solution)/shard_map/all_to_all | solution.py:464
  28.8 1.6 reshape.363.x_ref
  30.4 38.5 %shard_map.212 = bf16[4,2,256,2048]{3,2,1,0:T(8,128)(2,1)} custom-call(bf16[256,2048]{1,0:T(8,128)(2,1)} %reshape.363.x_ref), custom_call_target="tpu_custom_call" | custom-call | bytes 33554432 | tf_op jit(solution)/shard_map/pallas_call | solution.py:342
  68.9 5.1 multiply_reduce_fusion
  76.2 1.7 slice.94
  78.1 9.1 %multiply_convert_fusion = bf16[4,2,256,2048]{3,2,1,0:T(8,128)(2,1)} fusion(f32[2048]{0:T(1024)S(1)} %mul.269, f32[4,2,256]{2,1,0:T(2,128)S(1)} %get-tuple-element.80, bf16[4,2,256,2048]{3,2,1,0:T(8,128)(2,1)} %shard_map.212), kind=kLoop, calls=%fused_computation.4 | loop fusion | flops 16777216 | bytes 16793600 | tf_op jit(solution)/shard_map/convert_element_type | solution.py:520
  87.2 7.1 fusion.35.pre_ref
  98.1 2.1 reshape.368
  100.6 1.8 reshape.369
  102.3 4.7 reshape.370
  108.4 2.7 pad_maximum_fusion.1
  111.1 3.7 all-to-all-start.1
  114.8 54.9 %shard_map.213 = bf16[4,2,256,2048]{3,2,1,0:T(8,128)(2,1)} custom-call(bf16[256,2048]{1,0:T(8,128)(2,1)} %bitcast.148), custom_call_target="tpu_custom_call" | custom-call | bytes 33554432 | tf_op jit(solution)/shard_map/pallas_call | solution.py:342
  169.7 1.6 fusion.32
  175.6 36.9 %shard_map.214 = (bf16[4,2,2,128,256]{4,3,2,1,0:T(8,128)(2,1)}, bf16[4,2,2,128,256]{4,3,2,1,0:T(8,128)(2,1)}, f32[8,4,256]{2,1,0:T(4,128)}) custom-call(s32[33]{0:T(128)} %pad_add_fusion.1.scalars, f32[4,2,2,128,384]{4,3,2,1,0:T(8,128)} %copy-done.8, f32[256,256]{1,0:T(8,128)} %copy.95.cos_ref, f32[256,256]{1,0:T(8,128)} %copy.96.sin_ref, ...), custom_call_target="tpu_custom_call" | custom-call | flops 2147483648 | bytes 4194304 | tf_op jit(solution)/shard_map/pallas_call | solution.py:550
  212.4 6.8 convolution_convert_fusion.2
  219.3 41.4 %shard_map.215 = f32[256,2048]{1,0:T(8,128)} custom-call(bf16[4,2,256,2048]{3,2,1,0:T(8,128)(2,1)} %bitcast.147), custom_call_target="tpu_custom_call" | custom-call | bytes 33554432 | tf_op jit(solution)/shard_map/pallas_call | solution.py:368
  260.7 2.1 multiply_reduce_fusion.2
  264.2 2.6 reshape.374
  266.8 2.7 copy.98
  269.5 2.6 reshape.375.x_ref
  272.2 39.3 %shard_map.216 = bf16[4,2,256,2048]{3,2,1,0:T(8,128)(2,1)} custom-call(bf16[256,2048]{1,0:T(8,128)(2,1)} %reshape.375.x_ref), custom_call_target="tpu_custom_call" | custom-call | bytes 33554432 | tf_op jit(solution)/shard_map/pallas_call | solution.py:342
  311.6 11.5 %fusion.36 = f32[2048,704]{0,1:T(8,128)} fusion(bf16[2048,2048]{1,0:T(8,128)(2,1)} %bitcast.159, bf16[2048,704]{1,0:T(8,128)(2,1)} %all-gather.13.cloned.1.call-done), kind=kOutput, calls=%fused_computation.108 | convolution fusion | flops 5905580032 | bytes 17039360 | tf_op jit(solution)/shard_map/dot_general | solution.py:577
  323.1 12.8 %multiply_convert_fusion.1 = (bf16[2048,704]{0,1:T(8,128)(2,1)S(1)}, f32[2048,704]{0,1:T(8,128)}) fusion(f32[2048,704]{0,1:T(8,128)} %fusion.36, bf16[2048,2048]{1,0:T(8,128)(2,1)} %bitcast.160, bf16[2048,704]{1,0:T(8,128)(2,1)} %all-gather.15.cloned.1.call-done), kind=kOutput, calls=%fused_computation.16 | convolution fusion | flops 5914230784 | bytes 25690112 | tf_op jit(solution)/shard_map/dot_general | solution.py:578
  335.9 1.6 copy-done.32
  337.5 10.9 %convolution_convert_fusion.6 = bf16[704,2048]{1,0:T(8,128)(2,1)} fusion(bf16[2048,704]{0,1:T(8,128)(2,1)S(1)} %get-tuple-element.87, bf16[2048,2048]{1,0:T(8,128)(2,1)} %bitcast.157), kind=kOutput, calls=%fused_computation.21 | convolution fusion | flops 5907021824 | bytes 14155776 | tf_op jit(solution)/shard_map/dot_general | solution.py:583
  348.4 21.1 %all-gather.17.cloned.1.call-done = bf16[704,2048]{1,0:T(8,128)(2,1)} async-done(((bf16[176,2048]{1,0:T(8,128)(2,1)}), bf16[704,2048]{1,0:T(8,128)(2,1)}) %all-gather.17.cloned.1.call-update) | async-done | bytes 2883600 | tf_op jit(solution)/shard_map/all_gather | solution.py:467
  369.5 14.4 %fusion.4 = (bf16[2048,704]{0,1:T(8,128)(2,1)}, bf16[2048,704]{0,1:T(8,128)(2,1)S(1)}) fusion(f32[2048,704]{0,1:T(8,128)} %get-tuple-element.88, f32[2048,704]{0,1:T(8,128)} %fusion.36, bf16[2048,2048]{1,0:T(8,128)(2,1)} %bitcast.158, bf16[704,2048]{1,0:T(8,128)(2,1)} %all-gather.17.cloned.1.call-done), kind=kOutput, calls=%fused_computation.13 | convolution fusion | flops 5922881536 | bytes 28573696 | tf_op jit(solution)/shard_map/dot_general | solution.py:61
  383.9 1.6 copy-done.33
  385.5 12.0 %convolution_convert_fusion.3 = bf16[2048,704]{0,1:T(8,128)(2,1)} fusion(bf16[2048,2048]{1,0:T(8,128)(2,1)} %bitcast.161, f32[2048,704]{0,1:T(8,128)} %fusion.36, bf16[2048,704]{0,1:T(8,128)(2,1)S(1)} %get-tuple-element.90), kind=kOutput, calls=%fused_computation.18 | convolution fusion | flops 5917114368 | bytes 19922944 | tf_op jit(solution)/shard_map/dot_general | solution.py:583
  397.5 10.5 %convolution_convert_fusion.4 = bf16[2048,704]{0,1:T(8,128)(2,1)} fusion(bf16[2048,704]{0,1:T(8,128)(2,1)} %get-tuple-element.89, bf16[2048,2048]{1,0:T(8,128)(2,1)} %bitcast.162), kind=kOutput, calls=%fused_computation.19 | convolution fusion | flops 5907021824 | bytes 14155776 | tf_op jit(solution)/shard_map/dot_general | solution.py:583
  408.0 12.7 %fusion.37 = f32[2048,2048]{1,0:T(8,128)} fusion(bf16[2048,704]{0,1:T(8,128)(2,1)} %get-tuple-element.89, bf16[2048,704]{1,0:T(8,128)(2,1)} %all-gather.13.cloned.1.call-done), kind=kOutput, calls=%fused_computation.109 | convolution fusion | flops 5905580032 | bytes 22544384 | tf_op jit(solution)/shard_map/dot_general | solution.py:61
  420.7 16.7 %add_convert_fusion = bf16[2048,2048]{1,0:T(8,128)(2,1)} fusion(f32[2048,2048]{1,0:T(8,128)} %fusion.37, bf16[2048,704]{1,0:T(8,128)(2,1)} %all-gather.15.cloned.1.call-done, f32[2048,704]{0,1:T(8,128)} %fusion.36, bf16[2048,704]{0,1:T(8,128)(2,1)} %copy-done.33), kind=kOutput, calls=%fused_computation.3 | convolution fusion | flops 5924061184 | bytes 36700160 | tf_op jit(solution)/shard_map/dot_general | solution.py:61
  437.4 42.3 %shard_map.217 = f32[256,2048]{1,0:T(8,128)} custom-call(bf16[4,2,256,2048]{3,2,1,0:T(8,128)(2,1)} %bitcast.155), custom_call_target="tpu_custom_call" | custom-call | bytes 33554432 | tf_op jit(solution)/shard_map/pallas_call | solution.py:368
  479.8 2.3 multiply_reduce_fusion.1
  482.2 1.7 fusion.29.x_ref
  483.9 38.7 %shard_map.218 = bf16[4,2,256,2048]{3,2,1,0:T(8,128)(2,1)} custom-call(bf16[256,2048]{1,0:T(8,128)(2,1)} %fusion.29.x_ref), custom_call_target="tpu_custom_call" | custom-call | bytes 33554432 | tf_op jit(solution)/shard_map/pallas_call | solution.py:342
  522.6 7.0 convolution_convert_fusion.9
  529.6 36.5 %shard_map.219 = (bf16[4,2,2,128,256]{4,3,2,1,0:T(8,128)(2,1)}, bf16[8,1024,128]{2,1,0:T(8,128)(2,1)}) custom-call(s32[33]{0:T(128)} %pad_add_fusion.1.scalars, bf16[4,2,2,128,256]{4,3,2,1,0:T(8,128)(2,1)} %get-tuple-element.43.q_ref, bf16[4,2,2,128,256]{4,3,2,1,0:T(8,128)(2,1)} %bitcast.203, f32[256,256]{1,0:T(8,128)} %copy.95.cos_ref, ...), custom_call_target="tpu_custom_call" | custom-call | flops 5368709120 | bytes 4194304 | tf_op jit(solution)/shard_map/pallas_call | solution.py:614
  566.1 11.3 %convolution_convert_fusion.1 = bf16[2048,2048]{1,0:T(8,128)(2,1)} fusion(bf16[2048,704]{0,1:T(8,128)(2,1)} %copy-done.32, bf16[704,2048]{1,0:T(8,128)(2,1)} %all-gather.17.cloned.1.call-done), kind=kOutput, calls=%fused_computation.7 | convolution fusion | flops 5909774336 | bytes 14155776 | tf_op jit(solution)/shard_map/dot_general | solution.py:644
  579.5 9.0 %fusion.1 = bf16[2048,2048]{1,0:T(8,128)(2,1)} fusion(f32[2048]{0:T(1024)S(1)} %copy-done.24, f32[2048]{0:T(1024)S(1)} %bitcast.199, bf16[4,2,256,2048]{3,2,1,0:T(8,128)(2,1)} %shard_map.212), kind=kLoop, calls=%fused_computation.2 | loop fusion | flops 16777216 | bytes 16793600 | tf_op jit(solution)/shard_map/convert_element_type | solution.py:520
  588.5 41.7 %shard_map.220 = f32[256,2048]{1,0:T(8,128)} custom-call(bf16[4,2,256,2048]{3,2,1,0:T(8,128)(2,1)} %bitcast.151), custom_call_target="tpu_custom_call" | custom-call | bytes 33554432 | tf_op jit(solution)/shard_map/pallas_call | solution.py:368
  630.2 7.0 convolution_convert_fusion.8
  639.5 7.0 convolution_convert_fusion
  646.5 6.3 convolution_convert_fusion.7
  653.1 23.7 %reduce-scatter.15.cloned.1.call-done = bf16[512,704]{0,1:T(8,128)(2,1)} async-done(((bf16[2048,704]{0,1:T(8,128)(2,1)}), bf16[512,704]{0,1:T(8,128)(2,1)}) %reduce-scatter.15.cloned.1.call-update) | async-done | bytes 720912 | tf_op jit(solution)/shard_map/reduce_scatter | solution.py:588
  676.8 2.3 copy.107
  679.1 4.2 all-to-all-start.4
  683.5 47.4 %shard_map.221 = f32[256,2048]{1,0:T(8,128)} custom-call(bf16[4,2,256,2048]{3,2,1,0:T(8,128)(2,1)} %bitcast.154), custom_call_target="tpu_custom_call" | custom-call | bytes 33554432 | tf_op jit(solution)/shard_map/pallas_call | solution.py:368
  730.8 2.1 fusion.9
  732.9 2.3 reduce-scatter.13.cloned.1.call-done
  735.3 2.3 copy.106
  737.5 4.5 all-to-all-start.3
  742.0 6.5 fusion.13
  748.5 45.0 %reduce-scatter.17.cloned.1.call-done = bf16[176,2048]{1,0:T(8,128)(2,1)} async-done(((bf16[704,2048]{1,0:T(8,128)(2,1)}), bf16[176,2048]{1,0:T(8,128)(2,1)}) %reduce-scatter.17.cloned.1.call-update) | async-done | bytes 720912 | tf_op jit(solution)/shard_map/reduce_scatter | solution.py:588
  793.5 2.4 convert_element_type.202
  795.9 27.6 %reduce-scatter.11.cloned.1.call-done = bf16[64,2048]{1,0:T(8,128)(2,1)} async-done(((bf16[256,2048]{1,0:T(8,128)(2,1)}), bf16[64,2048]{1,0:T(8,128)(2,1)}) %reduce-scatter.11.cloned.1.call-update) | async-done | bytes 262160 | tf_op jit(solution)/shard_map/reduce_scatter | solution.py:588
  823.5 1.8 convert_element_type.197
  825.2 2.6 shard_map.223
  827.8 2.7 shard_map.222
  830.8 28.8 %reduce-scatter.9.cloned.1.call-done = bf16[512,384]{1,0:T(8,128)(2,1)} async-done(((bf16[2048,384]{1,0:T(8,128)(2,1)}), bf16[512,384]{1,0:T(8,128)(2,1)}) %reduce-scatter.9.cloned.1.call-update) | async-done | bytes 393232 | tf_op jit(solution)/shard_map/reduce_scatter | solution.py:588
  859.6 3.6 all-to-all-start.2
  863.2 1.6 multiply_reduce_fusion.4
  865.4 6.2 all-to-all-done.2
  (179 shorter events, 29.8 us)
Async XLA Ops:
  7.2 4.5 copy-start.20
  7.2 4.7 copy-start.27
  7.2 4.7 copy-start.29
  7.2 68.0 %all-gather.7.cloned.1.call-start = ((), (), s32[]{:S(2)}) async-start(), calls=%async_computation.11 | async-start | bytes 2457600 | tf_op jit(solution)/shard_map/all_gather | solution.py:467
  10.3 17.1 %copy-start.1 = (bf16[2,128,2048]{2,1,0:T(8,128)(2,1)S(1)}, bf16[2,128,2048]{2,1,0:T(8,128)(2,1)}, u32[]{:S(2)}) copy-start(bf16[2,128,2048]{2,1,0:T(8,128)(2,1)} %param.13) | copy-start | bytes 3145732
  26.6 71.4 %all-gather.9.cloned.1.call-start = ((), (), s32[]{:S(2)}) async-start(), calls=%async_computation.12 | async-start | bytes 1310720 | tf_op jit(solution)/shard_map/all_gather | solution.py:467
  27.4 142.4 %all-gather.11.cloned.1.call-start = ((), (), s32[]{:S(2)}) async-start(), calls=%async_computation.13 | async-start | bytes 2621440 | tf_op jit(solution)/shard_map/all_gather | solution.py:531
  75.2 19.3 %copy-start.12 = (f32[2,128,32]{2,1,0:T(8,128)}, f32[2,128,32]{2,1,0:T(8,128)S(1)}, u32[]{:S(2)}) copy-start(f32[2,128,32]{2,1,0:T(8,128)S(1)} %get-tuple-element.83) | copy-start | bytes 98308
  75.2 19.3 %copy-start.14 = (f32[2,128,32]{2,1,0:T(8,128)}, f32[2,128,32]{2,1,0:T(8,128)S(1)}, u32[]{:S(2)}) copy-start(f32[2,128,32]{2,1,0:T(8,128)S(1)} %get-tuple-element.84) | copy-start | bytes 98308
  77.9 9.2 %copy-start.10 = (bf16[4,4,2,64,384]{4,3,2,1,0:T(8,128)(2,1)}, bf16[4,4,2,64,384]{4,3,2,1,0:T(8,128)(2,1)S(1)}, u32[]{:S(2)}) copy-start(bf16[4,4,2,64,384]{4,3,2,1,0:T(8,128)(2,1)S(1)} %slice.94) | copy-start | bytes 4718596
  78.1 9.1 %copy-start.23 = (f32[2048]{0:T(1024)}, f32[2048]{0:T(1024)S(1)}, u32[]{:S(2)}) copy-start(f32[2048]{0:T(1024)S(1)} %mul.269) | copy-start | bytes 24580
  94.3 1.6 copy-start.8
  94.5 3.6 copy-start.6
  111.1 58.6 %all-to-all-start.1 = ((bf16[8,64,1408]{2,1,0:T(8,128)(2,1)}), bf16[8,64,1408]{2,1,0:T(8,128)(2,1)S(1)}, u32[]{:S(2)}, u32[]{:S(2)}) async-start(bf16[8,64,1408]{2,1,0:T(8,128)(2,1)} %pad_maximum_fusion.1), calls=%async_computation.1 | async-start | bytes 2883584 | tf_op jit(solution)/shard_map/all_to_all | solution.py:464
  114.8 196.8 %all-gather.13.cloned.1.call-start = ((), (), s32[]{:S(2)}) async-start(), calls=%async_computation.14 | async-start | bytes 3932160 | tf_op jit(solution)/shard_map/all_gather | solution.py:467
  171.4 151.7 %all-gather.15.cloned.1.call-start = ((), (), s32[]{:S(2)}) async-start(), calls=%async_computation.15 | async-start | bytes 3932160 | tf_op jit(solution)/shard_map/all_gather | solution.py:467
  172.0 197.5 %all-gather.17.cloned.1.call-start = ((), (), s32[]{:S(2)}) async-start(), calls=%async_computation.16 | async-start | bytes 3604480 | tf_op jit(solution)/shard_map/all_gather | solution.py:467
  175.6 36.9 %copy-start.17 = (bf16[256,2048]{1,0:T(8,128)(2,1)S(1)}, bf16[256,2048]{1,0:T(8,128)(2,1)}, u32[]{:S(2)}) copy-start(bf16[256,2048]{1,0:T(8,128)(2,1)} %all-gather.9.cloned.1.call-done) | copy-start | bytes 3145732
  260.7 2.3 copy-start
  311.5 318.7 %reduce-scatter.7.cloned.1.call-start = ((), (), s32[]{:S(2)}) async-start(), calls=%async_computation.17 | async-start | bytes 2621440 | tf_op jit(solution)/shard_map/reduce_scatter | solution.py:646
  335.9 1.6 copy-start.32
  383.9 1.6 copy-start.33
  479.7 2.3 copy-start.2
  479.7 2.5 copy-start.3
  577.4 99.5 %reduce-scatter.15.cloned.1.call-start = ((), (), s32[]{:S(2)}) async-start(), calls=%async_computation.21 | async-start | bytes 3604480 | tf_op jit(solution)/shard_map/reduce_scatter | solution.py:588
  578.1 1.4 copy-start.26
  578.1 1.4 copy-start.24
  578.1 157.1 %reduce-scatter.13.cloned.1.call-start = ((), (), s32[]{:S(2)}) async-start(), calls=%async_computation.20 | async-start | bytes 3604480 | tf_op jit(solution)/shard_map/reduce_scatter | solution.py:588
  578.9 214.6 %reduce-scatter.17.cloned.1.call-start = ((), (), s32[]{:S(2)}) async-start(), calls=%async_computation.22 | async-start | bytes 3604480 | tf_op jit(solution)/shard_map/reduce_scatter | solution.py:588
  579.5 244.0 %reduce-scatter.11.cloned.1.call-start = ((), (), s32[]{:S(2)}) async-start(), calls=%async_computation.19 | async-start | bytes 1310720 | tf_op jit(solution)/shard_map/reduce_scatter | solution.py:588
  637.3 1.7 copy-start.13
  637.3 1.7 copy-start.15
  637.3 222.3 %reduce-scatter.9.cloned.1.call-start = ((), (), s32[]{:S(2)}) async-start(), calls=%async_computation.18 | async-start | bytes 1966080 | tf_op jit(solution)/shard_map/reduce_scatter | solution.py:588
  637.4 2.1 copy-start.11
  637.4 2.1 copy-start.31
  639.0 7.5 slice-start
  639.5 7.0 slice-start.1
  652.8 30.5 %copy-start.25 = (f32[4,4,2,64]{3,2,0,1:T(2,128)S(1)}, f32[4,4,2,64]{3,2,0,1:T(2,128)}, u32[]{:S(2)}) copy-start(f32[4,4,2,64]{3,2,0,1:T(2,128)} %get-tuple-element.77) | copy-start | bytes 24580
  679.1 58.4 %all-to-all-start.4 = ((bf16[8,64,704]{2,1,0:T(8,128)(2,1)}), bf16[8,64,704]{2,1,0:T(8,128)(2,1)}, u32[]{:S(2)}, u32[]{:S(2)}) async-start(bf16[8,64,704]{2,1,0:T(8,128)(2,1)} %bitcast.169), calls=%async_computation.9 | async-start | bytes 1572864 | tf_op jit(solution)/shard_map/all_to_all | solution.py:592
  737.5 90.3 %all-to-all-start.3 = ((bf16[8,64,704]{2,1,0:T(8,128)(2,1)}), bf16[8,64,704]{2,1,0:T(8,128)(2,1)}, u32[]{:S(2)}, u32[]{:S(2)}) async-start(bf16[8,64,704]{2,1,0:T(8,128)(2,1)} %bitcast.168), calls=%async_computation.7 | async-start | bytes 1572864 | tf_op jit(solution)/shard_map/all_to_all | solution.py:592
  795.9 34.7 %copy-start.5 = (bf16[64,5632]{1,0:T(8,128)(2,1)S(1)}, bf16[64,5632]{1,0:T(8,128)(2,1)}, u32[]{:S(2)}) copy-start(bf16[64,5632]{1,0:T(8,128)(2,1)} %param.21) | copy-start | bytes 2162692
  827.8 2.7 copy-start.4
  827.8 35.4 %copy-start.7 = (bf16[64,5632]{1,0:T(8,128)(2,1)S(1)}, bf16[64,5632]{1,0:T(8,128)(2,1)}, u32[]{:S(2)}) copy-start(bf16[64,5632]{1,0:T(8,128)(2,1)} %param.20) | copy-start | bytes 2162692
  830.5 34.3 %copy-start.30 = (bf16[64]{0:T(256)(128)(2,1)S(1)}, bf16[64]{0:T(256)(128)(2,1)}, u32[]{:S(2)}) copy-start(bf16[64]{0:T(256)(128)(2,1)} %param.23) | copy-start | bytes 388
  859.6 11.9 %all-to-all-start.2 = ((bf16[8,64,384]{2,1,0:T(8,128)(2,1)}), bf16[8,64,384]{2,1,0:T(8,128)(2,1)S(1)}, u32[]{:S(2)}, u32[]{:S(2)}) async-start(bf16[8,64,384]{2,1,0:T(8,128)(2,1)} %bitcast.193), calls=%async_computation.4 | async-start | bytes 786432 | tf_op jit(solution)/shard_map/all_to_all | solution.py:592
  872.0 2.7 copy-start.18
  872.2 2.5 copy-start.19
  872.2 2.3 copy-start.16
  872.2 2.4 copy-start.21
  872.3 2.4 copy-start.22
  872.3 2.6 copy-start.28
  874.5 0.8 copy-start.9
Sparse Core Ops, SparseCore 0:
  26.7 42.8 all-gather.6
  71.2 26.8 all-gather.8
  100.2 45.0 all-gather.10
  171.5 62.2 all-gather.12
  235.2 62.0 all-gather.14
  311.6 57.8 all-gather.16
  577.5 41.4 reduce-scatter.6
  621.3 55.5 reduce-scatter.14
  679.2 56.0 reduce-scatter.12
  737.4 56.0 reduce-scatter.16
  796.4 27.0 reduce-scatter.10
  825.6 33.9 reduce-scatter.8

commit v3 on v2

--- a/solution.py
+++ b/solution.py
@@ -314,6 +314,249 @@
         copy.wait_send()
 
 
+def blocks_of(values, order):
+    block = values.shape[1] // len(order)
+    return jnp.concatenate(
+        [values[:, source * block : (source + 1) * block] for source in order], axis=1
+    )
+
+
+def pivot_kernel(
+    nd,
+    forward,
+    orders_out,
+    part_ref,
+    own_ref,
+    gain_ref,
+    *rest,
+):
+    middle_ref = None
+    if not forward:
+        middle_ref, rest = rest[0], rest[1:]
+    (
+        row_ref,
+        group_ref,
+        mine,
+        from_core,
+        out_box,
+        in_box,
+        held,
+        load_sem,
+        send,
+        recv,
+        core_send,
+        core_recv,
+        keep_sem,
+        send2,
+        recv2,
+        core_send2,
+        core_recv2,
+    ) = rest
+    dp, core = lax.axis_index("dp"), lax.axis_index("core")
+    other = 1 - core
+    rows = row_ref.shape[0] // (PARTS * CHUNKS)
+    greet(nd, dp, other)
+    orders = hops(nd)
+    pieces = [(c, p) for c in range(CHUNKS) for p in range(PARTS)]
+
+    def span(c, p):
+        return pl.ds((p * CHUNKS + c) * rows, rows)
+
+    def slot(c, p, mask):
+        return (p * CHUNKS + c) * nd + mask
+
+    def share(c, p, mask):
+        index = slot(c, p, mask)
+        return pltpu.make_async_remote_copy(
+            src_ref=part_ref.at[flip(dp, mask), other, span(c, p)],
+            dst_ref=from_core.at[mask, span(c, p)],
+            send_sem=core_send.at[index],
+            recv_sem=core_recv.at[index],
+            device_id={"core": other},
+            device_id_type=MESH,
+        )
+
+    def hop(c, p, mask):
+        index = slot(c, p, mask)
+        bit = next(bit for bit in orders[p] if mask & bit)
+        return pltpu.make_async_remote_copy(
+            src_ref=out_box.at[mask, span(c, p)],
+            dst_ref=in_box.at[mask, span(c, p)],
+            send_sem=send.at[index],
+            recv_sem=recv.at[index],
+            device_id={"dp": flip(dp, bit)},
+            device_id_type=MESH,
+        )
+
+    def hop_out(c, p, mask, bit):
+        place = group_ref.at[flip(dp, mask), core, span(c, p)]
+        index = slot(c, p, mask + bit)
+        return pltpu.make_async_remote_copy(
+            src_ref=held.at[span(c, p)] if mask == 0 else place,
+            dst_ref=place,
+            send_sem=send2.at[index],
+            recv_sem=recv2.at[index],
+            device_id={"dp": flip(dp, bit)},
+            device_id_type=MESH,
+        )
+
+    def share_out(c, p, mask):
+        place = group_ref.at[flip(dp, mask), core, span(c, p)]
+        index = slot(c, p, mask)
+        return pltpu.make_async_remote_copy(
+            src_ref=held.at[span(c, p)] if mask == 0 else place,
+            dst_ref=place,
+            send_sem=core_send2.at[index],
+            recv_sem=core_recv2.at[index],
+            device_id={"core": other},
+            device_id_type=MESH,
+        )
+
+    def stage(p, mask):
+        order = orders[p]
+        return next((i for i, bit in enumerate(order) if mask & bit), len(order))
+
+    steps = []
+    for position in range(len(orders[0]) + 1):
+        for c, p in pieces:
+            masks = [m for m in range(nd - 1, -1, -1) if stage(p, m) == position]
+            steps += [(c, p, m) for m in masks]
+    started = []
+    for c, p, mask in steps:
+        copy = share(c, p, mask)
+        copy.start()
+        started.append(copy)
+    loads = [
+        pltpu.make_async_copy(part_ref.at[flip(dp, mask), core], mine.at[mask], load_sem.at[mask])
+        for mask in range(nd)
+    ]
+    for load in loads:
+        load.start()
+    for load in loads:
+        load.wait()
+    step_rows = 16
+    gain = gain_ref[...]
+    kept = []
+
+    def finish(total, at):
+        if forward:
+            middle = own_ref[at].astype(f32) + total
+            inverse = rms_scale(middle)
+            row_ref[at] = middle
+            held[at] = blocks_of((middle * inverse * gain).astype(bf16), orders_out)
+            return
+        middle = middle_ref[at]
+        inverse = rms_scale(middle)
+        grad = own_ref[at].astype(f32) + rms_back(
+            blocks_of(total, orders_out), middle, inverse, gain
+        )
+        row_ref[at] = grad
+        held[at] = grad.astype(bf16)
+
+    for c, p, mask in steps:
+        order = orders[p]
+        arrived = [mask + bit for bit in order[: stage(p, mask)]]
+        share(c, p, mask).wait_recv()
+        for m in arrived:
+            hop(c, p, m).wait_recv()
+        first = (p * CHUNKS + c) * rows
+
+        def add(i, carry, mask=mask, arrived=arrived, first=first):
+            at = pl.ds(pl.multiple_of(first + i * step_rows, step_rows), step_rows)
+            total = mine[mask, at].astype(f32) + from_core[mask, at].astype(f32)
+            for m in arrived:
+                total = total + in_box[m, at].astype(f32)
+            if mask == 0:
+                finish(total, at)
+            else:
+                out_box[mask, at] = total.astype(bf16)
+            return carry
+
+        lax.fori_loop(0, rows // step_rows, add, 0)
+        copies = [hop(c, p, mask)] if mask else []
+        if mask == 0:
+            copies = [hop_out(c, p, 0, bit) for bit in order] + [share_out(c, p, 0)]
+            keep = pltpu.make_async_copy(
+                held.at[span(c, p)],
+                group_ref.at[dp, core, span(c, p)],
+                keep_sem.at[p * CHUNKS + c],
+            )
+            keep.start()
+            kept.append(keep)
+        for copy in copies:
+            copy.start()
+            started.append(copy)
+    for size in range(1, len(orders[0]) + 1):
+        for c, p in pieces:
+            order = orders[p]
+            for mask in range(1, nd):
+                if bin(mask).count("1") != size:
+                    continue
+                last = max(i for i, bit in enumerate(order) if mask & bit)
+                hop_out(c, p, mask - order[last], order[last]).wait_recv()
+                copies = [hop_out(c, p, mask, bit) for bit in order[last + 1 :]]
+                for copy in copies + [share_out(c, p, mask)]:
+                    copy.start()
+                    started.append(copy)
+    for c, p in pieces:
+        for mask in range(nd):
+            share_out(c, p, mask).wait_recv()
+    for copy in started:
+        copy.wait_send()
+    for keep in kept:
+        keep.wait()
+
+
+def plane_pivot(part, own, gain, middle, nd, nc, ident, order):
+    rows, width = own.shape
+    sems = PARTS * CHUNKS * nd
+    box = pltpu.VMEM((nd, rows, width), bf16)
+    dma = pltpu.SemaphoreType.DMA
+    whole = pl.BlockSpec(memory_space=pltpu.VMEM)
+    extra = () if middle is None else (middle,)
+    out, group = pl.pallas_call(
+        functools.partial(pivot_kernel, nd, middle is None, tuple(order)),
+        out_shape=(
+            jax.ShapeDtypeStruct((rows, width), f32),
+            jax.ShapeDtypeStruct((nd, nc, rows, width), bf16),
+        ),
+        in_specs=[pl.BlockSpec(memory_space=pl.ANY)] + [whole] * (2 + len(extra)),
+        out_specs=(whole, pl.BlockSpec(memory_space=pl.ANY)),
+        scratch_shapes=[box, box, box, box, pltpu.VMEM((rows, width), bf16), dma((nd,))]
+        + [dma((sems,))] * 4
+        + [dma((PARTS * CHUNKS,))]
+        + [dma((sems,))] * 4,
+        compiler_params=pltpu.CompilerParams(collective_id=ident, has_side_effects=True),
+        cost_estimate=pl.CostEstimate(
+            flops=0, bytes_accessed=32 * nd * rows * width, transcendentals=0
+        ),
+    )(part.reshape(nd, nc, rows, width), own, gain.reshape(1, width), *extra)
+    return out, group.reshape(nd * nc * rows, width)
+
+
+def split_kernel(nd, nz, nc, unit, gate_ref, up_ref, out_ref):
+    for g, weight_ref in enumerate((gate_ref, up_ref)):
+        weight = weight_ref[...].astype(f32)
+        for d in range(nd):
+            for c in range(nc):
+                for z in range(nz):
+                    at = ((d * nz + z) * nc + c) * unit
+                    to = (g * nz + z) * unit
+                    out_ref[d * nc + c, :, to : to + unit] = weight[:, at : at + unit].astype(bf16)
+
+
+def split_columns(gate, up, nd, nz, nc, unit):
+    held = gate.shape[0]
+    whole = pl.BlockSpec(memory_space=pltpu.VMEM)
+    return pl.pallas_call(
+        functools.partial(split_kernel, nd, nz, nc, unit),
+        out_shape=jax.ShapeDtypeStruct((nd * nc, held, 2 * nz * unit), bf16),
+        in_specs=[whole, whole],
+        out_specs=whole,
+        cost_estimate=pl.CostEstimate(flops=0, bytes_accessed=8 * gate.size, transcendentals=0),
+    )(gate, up)
+
+
 def place_kernel(nd, nz, nc, unit, parts_ref, out_ref):
     for d in range(nd):
         for c in range(nc):
@@ -500,9 +743,7 @@
     else:
         wo = lax.all_gather(w_output, ("zz", "core"), axis=0, tiled=True)
         wo = lax.dynamic_slice_in_dim(wo, core * q_width, q_width, 0)
-    ff_columns = to_members(
-        jnp.concatenate([by_member(w_gate, ff_held), by_member(w_up, ff_held)], axis=-1)
-    )
+    ff_columns = to_members(split_columns(w_gate, w_up, nd, nz, nc, ff_held))
 
     positions = (zz * queries + jnp.arange(queries, dtype=jnp.int32)).astype(f32)
     frequency = rope_base ** (-jnp.arange(HALF, dtype=f32) / HALF)
@@ -568,12 +809,14 @@
     )(scalars, pre, cos_wide, sin_wide, kv_all)
 
     attended = attended.reshape(group, q_width)
-    mixed = reduce(jnp.dot(attended, wo, preferred_element_type=f32).astype(bf16), 5)
-    middle = x + mixed
-    inverse_mlp = rms_scale(middle)
-    normed_mid = gather(
-        to_weight_order((middle * inverse_mlp * gain_m).astype(bf16)), 3
-    )
+    mixed = jnp.dot(attended, wo, preferred_element_type=f32).astype(bf16)
+    if feature_block % 128:
+        middle = x + reduce(mixed, 5)
+        inverse_mlp = rms_scale(middle)
+        normed_mid = gather(to_weight_order((middle * inverse_mlp * gain_m).astype(bf16)), 3)
+    else:
+        order = [d * nz + z for z in range(nz) for d in range(nd)]
+        middle, normed_mid = plane_pivot(mixed, x_low, gain_m, None, nd, nc, 5, order)
     gate = jnp.dot(normed_mid, wg, preferred_element_type=f32)
     up = jnp.dot(normed_mid, wu, preferred_element_type=f32)
     sigmoid = jax.nn.sigmoid(gate)
@@ -599,16 +842,19 @@
     weight_gate = columns_dot(normed_mid, grad_gate)
     weight_up = columns_dot(normed_mid, grad_up)
     back_mid = (rows_dot(grad_gate, wg) + rows_dot(grad_up, wu)).astype(bf16)
-    back_mid, weight_gate, weight_up = tie((back_mid, weight_gate, weight_up))
     weight_gate = z_reduce(weight_gate)
     weight_up = z_reduce(weight_up)
     weight_gate = place_columns(home(weight_gate), nd, nz, nc, ff_held)
     weight_up = place_columns(home(weight_up), nd, nz, nc, ff_held)
 
-    grad_normed_mid = reduce_features(back_mid, 6)
-    grad_middle_norm = rms_back(grad_normed_mid, middle, inverse_mlp, gain_m)
-    grad_middle = dy_low.astype(f32) + grad_middle_norm
-    mid_group = gather(grad_middle.astype(bf16), 4)
+    if feature_block % 128:
+        grad_middle = dy_low.astype(f32) + rms_back(
+            reduce_features(back_mid, 6), middle, inverse_mlp, gain_m
+        )
+        mid_group = gather(grad_middle.astype(bf16), 4)
+    else:
+        order = [z * nd + d for d in range(nd) for z in range(nz)]
+        grad_middle, mid_group = plane_pivot(back_mid, dy_low, gain_m, middle, nd, nc, 6, order)
     grad_mix = rows_dot(mid_group, wo).astype(bf16)
 
     dq, dkv = pl.pallas_call(

time: 891 us -> 839 us (0.942)
  local copies, waits for them, and re-layouts: 45.3 us -> 28.8 us
  waiting for transfers between devices: 159 us -> 144 us
  other arithmetic: 54.7 us -> 42.9 us
    pallas_call x0 -> x3, Pallas kernels: none -> 162 us  [the longest x2 159 us: plane_pivot(): pl.pallas_call(functools.partial(pivot_kernel, nd, middle is None, tuple(...]
    pallas_call x4 -> x2, Pallas kernels: 173 us -> 83 us  [plane_reduce(): pl.pallas_call(functools.partial(collect_kernel, nd, tuple(order)), out_s...]
    pallas_call x4 -> x2, Pallas kernels: 171 us -> 92.9 us  [plane_gather(): pl.pallas_call(functools.partial(spread_kernel, nd), out_shape=jax.ShapeD...]
    reduce_scatter x5, waiting for transfers between devices: 127 us -> 111 us  [z_reduce(): return lax.psum_scatter(values, 'zz', scatter_dimension=0, tiled=True)]
  transfers between devices with their start and end apart: 16 -> 16, of which waited for: 8 -> 7; matrix products, arithmetic and copies ran while one was open for 17% -> 18% of each run, Pallas kernels for 35% -> 36%
where the time goes in v3:
time: 839 us; the launch traced here: 829 us
  Pallas kernels  416 us (50%)
  matrix products  151 us (18%)
  waiting for transfers between devices  144 us (17%)
  other arithmetic  42.9 us (5%)
  local copies, waits for them, and re-layouts  28.8 us (3%)
  starting transfers between devices  17.2 us (2%)
  between operations  15.2 us (2%)
  blocking collectives  14.5 us (2%)
    pallas_call x2, Pallas kernels, plane_pivot(): pl.pallas_call(functools.partial(pivot_kernel, nd, middle is None, tuple(...  159 us
    reduce_scatter x5, waiting for transfers between devices, z_reduce(): return lax.psum_scatter(values, 'zz', scatter_dimension=0, tiled=True)  111 us
    pallas_call x2, Pallas kernels, plane_gather(): pl.pallas_call(functools.partial(spread_kernel, nd), out_shape=jax.ShapeD...  92.9 us
    pallas_call x2, Pallas kernels, plane_reduce(): pl.pallas_call(functools.partial(collect_kernel, nd, tuple(order)), out_s...  83 us
    dot_general x5, matrix products, rows_dot(): lax.dot_general(left, right, (((1,), (1,)), ((), ())), preferred_element_...  55.1 us
    dot_general x5, matrix products, columns_dot(): lax.dot_general(left, right, (((0,), (0,)), ((), ())), preferred_element_...  47.8 us
    pallas_call x1, Pallas kernels, local(): pl.pallas_call(functools.partial(attend_kernel, pics, seqs, heads), out_s...  36.5 us
    pallas_call x1, Pallas kernels, local(): pl.pallas_call(functools.partial(attend_back_kernel, pics, seqs, heads),...  36.5 us
  transfers between devices with their start and end apart: 16, of which 7 were waited for; matrix products, arithmetic and copies ran while one was open for 18% of the time, Pallas kernels for 36%

profile of v3, /device:TPU:0, one launch (start us, length us, event | category | flops | bytes accessed | tf_op | source)
XLA Modules:
  0.0 829.4 jit_solution(5522247900327133452)
XLA Ops:
  7.2 0.8 reshape.327
  8.9 1.5 reshape.321
  10.9 0.9 reshape.323
  11.8 0.9 reshape.325
  13.6 14.5 %all_to_all.25 = bf16[8,80,384]{2,1,0:T(8,128)(2,1)} all-to-all(bf16[8,80,384]{2,1,0:T(8,128)(2,1)S(1)} %fusion.8), channel_id=1, replica_groups=mesh['dp'=4,'zz'=4,'core'=2] {'dp','core'}, dimensions={0} | all-to-all | bytes 983040 | tf_op jit(solution)/shard_map/all_to_all | solution.py:707
  30.2 1.6 reshape.332.x_ref
  31.8 38.5 %shard_map.212 = bf16[4,2,256,2048]{3,2,1,0:T(8,128)(2,1)} custom-call(bf16[256,2048]{1,0:T(8,128)(2,1)} %reshape.332.x_ref), custom_call_target="tpu_custom_call" | custom-call | bytes 33554432 | tf_op jit(solution)/shard_map/pallas_call | solution.py:585
  70.4 5.1 multiply_reduce_fusion
  76.7 1.0 slice.90
  77.7 1.7 slice.94
  79.5 9.1 %multiply_convert_fusion = bf16[4,2,256,2048]{3,2,1,0:T(8,128)(2,1)} fusion(f32[2048]{0:T(1024)S(1)} %mul.221, f32[4,2,256]{2,1,0:T(2,128)S(1)} %get-tuple-element.80, bf16[4,2,256,2048]{3,2,1,0:T(8,128)(2,1)} %shard_map.212), kind=kLoop, calls=%fused_computation.4 | loop fusion | flops 16777216 | bytes 16793600 | tf_op jit(solution)/shard_map/convert_element_type | solution.py:761
  88.6 6.9 fusion.26.pre_ref
  97.1 0.8 copy.83
  98.0 1.5 all-gather.9.cloned.1.call-done
  99.5 3.1 shard_map.214
  102.6 3.7 all-to-all-start.1
  106.9 54.4 %shard_map.213 = bf16[4,2,256,2048]{3,2,1,0:T(8,128)(2,1)} custom-call(bf16[256,2048]{1,0:T(8,128)(2,1)} %bitcast.119), custom_call_target="tpu_custom_call" | custom-call | bytes 33554432 | tf_op jit(solution)/shard_map/pallas_call | solution.py:585
  161.3 1.6 fusion.23
  163.8 0.8 copy.84.cos_ref
  164.6 0.8 copy.85.sin_ref
  167.7 36.5 %shard_map.215 = (bf16[4,2,2,128,256]{4,3,2,1,0:T(8,128)(2,1)}, bf16[4,2,2,128,256]{4,3,2,1,0:T(8,128)(2,1)}, f32[8,4,256]{2,1,0:T(4,128)}) custom-call(s32[33]{0:T(128)} %pad_add_fusion.1.scalars, f32[4,2,2,128,384]{4,3,2,1,0:T(8,128)} %copy-done.7, f32[256,256]{1,0:T(8,128)} %copy.84.cos_ref, f32[256,256]{1,0:T(8,128)} %copy.85.sin_ref, ...), custom_call_target="tpu_custom_call" | custom-call | flops 2147483648 | bytes 4194304 | tf_op jit(solution)/shard_map/pallas_call | solution.py:791
  204.2 6.8 convolution_convert_fusion.2
  211.3 78.6 %shard_map.216 = (f32[256,2048]{1,0:T(8,128)}, bf16[4,2,256,2048]{3,2,1,0:T(8,128)(2,1)}) custom-call(bf16[4,2,256,2048]{3,2,1,0:T(8,128)(2,1)} %bitcast.105, bf16[256,2048]{1,0:T(8,128)(2,1)} %bitcast.106, f32[1,2048]{1,0:T(1,128)} %reshape_reshape.8.gain_ref), custom_call_target="tpu_custom_call" | custom-call | bytes 67108864 | tf_op jit(solution)/shard_map/pallas_call | solution.py:517
  289.9 11.1 %fusion.27 = f32[2048,704]{0,1:T(8,128)} fusion(bf16[2048,2048]{1,0:T(8,128)(2,1)} %bitcast.156, bf16[2048,704]{1,0:T(8,128)(2,1)} %all-gather.13.cloned.1.call-done), kind=kOutput, calls=%fused_computation.91 | convolution fusion | flops 5905580032 | bytes 17039360 | tf_op jit(solution)/shard_map/dot_general | solution.py:820
  301.1 12.7 %multiply_convert_fusion.1 = (bf16[2048,704]{0,1:T(8,128)(2,1)S(1)}, f32[2048,704]{0,1:T(8,128)}) fusion(f32[2048,704]{0,1:T(8,128)} %fusion.27, bf16[2048,2048]{1,0:T(8,128)(2,1)} %bitcast.157, bf16[2048,704]{1,0:T(8,128)(2,1)} %all-gather.15.cloned.1.call-done), kind=kOutput, calls=%fused_computation.16 | convolution fusion | flops 5914230784 | bytes 25690112 | tf_op jit(solution)/shard_map/dot_general | solution.py:821
  313.8 1.6 copy-done.33
  315.3 10.9 %convolution_convert_fusion.6 = bf16[704,2048]{1,0:T(8,128)(2,1)} fusion(bf16[2048,704]{0,1:T(8,128)(2,1)S(1)} %get-tuple-element.87, bf16[2048,2048]{1,0:T(8,128)(2,1)} %bitcast.116), kind=kOutput, calls=%fused_computation.21 | convolution fusion | flops 5907021824 | bytes 14155776 | tf_op jit(solution)/shard_map/dot_general | solution.py:826
  326.2 22.2 %all-gather.17.cloned.1.call-done = bf16[704,2048]{1,0:T(8,128)(2,1)} async-done(((bf16[176,2048]{1,0:T(8,128)(2,1)}), bf16[704,2048]{1,0:T(8,128)(2,1)}) %all-gather.17.cloned.1.call-update) | async-done | bytes 2883600 | tf_op jit(solution)/shard_map/all_gather | solution.py:710
  348.5 14.5 %fusion.4 = (bf16[2048,704]{0,1:T(8,128)(2,1)S(1)}, bf16[2048,704]{0,1:T(8,128)(2,1)}) fusion(f32[2048,704]{0,1:T(8,128)} %get-tuple-element.88, f32[2048,704]{0,1:T(8,128)} %fusion.27, bf16[2048,2048]{1,0:T(8,128)(2,1)} %bitcast.117, bf16[704,2048]{1,0:T(8,128)(2,1)} %all-gather.17.cloned.1.call-done), kind=kOutput, calls=%fused_computation.13 | convolution fusion | flops 5922881536 | bytes 28573696 | tf_op jit(solution)/shard_map/dot_general | solution.py:61
  363.0 10.4 %fusion.28 = f32[2048,2048]{1,0:T(8,128)} fusion(bf16[2048,704]{0,1:T(8,128)(2,1)S(1)} %get-tuple-element.89, bf16[2048,704]{1,0:T(8,128)(2,1)S(1)} %copy-done.28), kind=kOutput, calls=%fused_computation.92 | convolution fusion | flops 5905580032 | bytes 22544384 | tf_op jit(solution)/shard_map/dot_general | solution.py:61
  373.3 16.3 %add_convert_fusion = bf16[2048,2048]{1,0:T(8,128)(2,1)} fusion(f32[2048,2048]{1,0:T(8,128)} %fusion.28, bf16[2048,704]{1,0:T(8,128)(2,1)} %all-gather.15.cloned.1.call-done, f32[2048,704]{0,1:T(8,128)} %fusion.27, bf16[2048,704]{0,1:T(8,128)(2,1)} %get-tuple-element.90), kind=kOutput, calls=%fused_computation.3 | convolution fusion | flops 5924061184 | bytes 36700160 | tf_op jit(solution)/shard_map/dot_general | solution.py:61
  389.6 80.3 %shard_map.217 = (f32[256,2048]{1,0:T(8,128)}, bf16[4,2,256,2048]{3,2,1,0:T(8,128)(2,1)}) custom-call(bf16[4,2,256,2048]{3,2,1,0:T(8,128)(2,1)} %bitcast.118, bf16[256,2048]{1,0:T(8,128)(2,1)} %bitcast.120, f32[1,2048]{1,0:T(1,128)} %reshape_reshape.8.gain_ref, f32[256,2048]{1,0:T(8,128)} %get-tuple-element.42.rest_0_), custom_call_target="tpu_custom_call" | custom-call | bytes 67108864 | tf_op jit(solution)/shard_map/pallas_call | solution.py:517
  469.9 6.7 convolution_convert_fusion.9
  476.6 36.5 %shard_map.218 = (bf16[4,2,2,128,256]{4,3,2,1,0:T(8,128)(2,1)}, bf16[8,1024,128]{2,1,0:T(8,128)(2,1)}) custom-call(s32[33]{0:T(128)} %pad_add_fusion.1.scalars, bf16[4,2,2,128,256]{4,3,2,1,0:T(8,128)(2,1)} %get-tuple-element.46.q_ref, bf16[4,2,2,128,256]{4,3,2,1,0:T(8,128)(2,1)} %bitcast.162, f32[256,256]{1,0:T(8,128)} %copy.84.cos_ref, ...), custom_call_target="tpu_custom_call" | custom-call | flops 5368709120 | bytes 4194304 | tf_op jit(solution)/shard_map/pallas_call | solution.py:860
  513.1 10.8 %convolution_convert_fusion.1 = bf16[2048,2048]{1,0:T(8,128)(2,1)} fusion(bf16[2048,704]{0,1:T(8,128)(2,1)} %copy-done.33, bf16[704,2048]{1,0:T(8,128)(2,1)S(1)} %copy-done.29), kind=kOutput, calls=%fused_computation.7 | convolution fusion | flops 5909774336 | bytes 14155776 | tf_op jit(solution)/shard_map/dot_general | solution.py:890
  524.0 12.9 %convolution_convert_fusion.3 = bf16[2048,704]{0,1:T(8,128)(2,1)} fusion(bf16[2048,2048]{1,0:T(8,128)(2,1)} %bitcast.158, f32[2048,704]{0,1:T(8,128)} %fusion.27, bf16[2048,704]{0,1:T(8,128)(2,1)} %get-tuple-element.90), kind=kOutput, calls=%fused_computation.18 | convolution fusion | flops 5917114368 | bytes 19922944 | tf_op jit(solution)/shard_map/dot_general | solution.py:826
  537.0 10.9 %convolution_convert_fusion.4 = bf16[2048,704]{0,1:T(8,128)(2,1)} fusion(bf16[2048,704]{0,1:T(8,128)(2,1)S(1)} %copy-done.32, bf16[2048,2048]{1,0:T(8,128)(2,1)} %bitcast.159), kind=kOutput, calls=%fused_computation.19 | convolution fusion | flops 5907021824 | bytes 14155776 | tf_op jit(solution)/shard_map/dot_general | solution.py:826
  548.6 8.6 %fusion.1 = bf16[2048,2048]{1,0:T(8,128)(2,1)} fusion(f32[2048]{0:T(1024)S(1)} %copy-done.23, f32[2048]{0:T(1024)S(1)} %bitcast.154, bf16[4,2,256,2048]{3,2,1,0:T(8,128)(2,1)} %shard_map.212), kind=kLoop, calls=%fused_computation.2 | loop fusion | flops 16777216 | bytes 16793600 | tf_op jit(solution)/shard_map/convert_element_type | solution.py:761
  557.2 41.5 %shard_map.219 = f32[256,2048]{1,0:T(8,128)} custom-call(bf16[4,2,256,2048]{3,2,1,0:T(8,128)(2,1)} %bitcast.111), custom_call_target="tpu_custom_call" | custom-call | bytes 33554432 | tf_op jit(solution)/shard_map/pallas_call | solution.py:611
  598.8 6.8 convolution_convert_fusion.8
  607.5 7.2 convolution_convert_fusion
  614.7 6.3 convolution_convert_fusion.7
  621.5 41.4 %shard_map.220 = f32[256,2048]{1,0:T(8,128)} custom-call(bf16[4,2,256,2048]{3,2,1,0:T(8,128)(2,1)} %bitcast.114), custom_call_target="tpu_custom_call" | custom-call | bytes 33554432 | tf_op jit(solution)/shard_map/pallas_call | solution.py:611
  662.9 2.4 copy.95
  665.3 4.2 all-to-all-start.4
  670.1 1.1 copy-done.4
  671.2 2.8 add_convert_fusion.2
  674.1 7.8 reduce-scatter.13.cloned.1.call-done
  681.9 2.3 copy.94
  684.2 4.2 all-to-all-start.3
  688.4 3.4 add_convert_fusion.1
  691.8 48.4 %reduce-scatter.17.cloned.1.call-done = bf16[176,2048]{1,0:T(8,128)(2,1)} async-done(((bf16[704,2048]{1,0:T(8,128)(2,1)}), bf16[176,2048]{1,0:T(8,128)(2,1)}) %reduce-scatter.17.cloned.1.call-update) | async-done | bytes 720912 | tf_op jit(solution)/shard_map/reduce_scatter | solution.py:831
  740.2 2.4 convert_element_type.186
  742.5 27.6 %reduce-scatter.11.cloned.1.call-done = bf16[64,2048]{1,0:T(8,128)(2,1)} async-done(((bf16[256,2048]{1,0:T(8,128)(2,1)}), bf16[64,2048]{1,0:T(8,128)(2,1)}) %reduce-scatter.11.cloned.1.call-update) | async-done | bytes 262160 | tf_op jit(solution)/shard_map/reduce_scatter | solution.py:831
  770.1 1.8 convert_element_type.179
  771.9 2.6 shard_map.222
  774.5 2.7 shard_map.221
  777.1 1.5 multiply_reduce_fusion.3
  778.6 27.6 %reduce-scatter.9.cloned.1.call-done = bf16[512,384]{1,0:T(8,128)(2,1)} async-done(((bf16[2048,384]{1,0:T(8,128)(2,1)}), bf16[512,384]{1,0:T(8,128)(2,1)}) %reduce-scatter.9.cloned.1.call-update) | async-done | bytes 393232 | tf_op jit(solution)/shard_map/reduce_scatter | solution.py:831
  806.2 3.9 all-to-all-start.2
  810.2 1.4 multiply_reduce_fusion.4
  812.0 6.4 all-to-all-done.2
  819.6 0.8 copy.106
  820.4 1.0 reshape.354
  (163 shorter events, 17.3 us)
Async XLA Ops:
  7.2 21.7 %copy-start = (bf16[2,128,2048]{2,1,0:T(8,128)(2,1)S(1)}, bf16[2,128,2048]{2,1,0:T(8,128)(2,1)}, u32[]{:S(2)}) copy-start(bf16[2,128,2048]{2,1,0:T(8,128)(2,1)} %param.13) | copy-start | bytes 3145732
  7.2 69.5 %all-gather.7.cloned.1.call-start = ((), (), s32[]{:S(2)}) async-start(), calls=%async_computation.11 | async-start | bytes 2457600 | tf_op jit(solution)/shard_map/all_gather | solution.py:710
  28.1 71.4 %all-gather.9.cloned.1.call-start = ((), (), s32[]{:S(2)}) async-start(), calls=%async_computation.12 | async-start | bytes 1310720 | tf_op jit(solution)/shard_map/all_gather | solution.py:710
  28.8 132.4 %all-gather.11.cloned.1.call-start = ((), (), s32[]{:S(2)}) async-start(), calls=%async_computation.13 | async-start | bytes 2621440 | tf_op jit(solution)/shard_map/all_gather | solution.py:772
  76.6 19.1 %copy-start.11 = (f32[2,128,32]{2,1,0:T(8,128)}, f32[2,128,32]{2,1,0:T(8,128)S(1)}, u32[]{:S(2)}) copy-start(f32[2,128,32]{2,1,0:T(8,128)S(1)} %get-tuple-element.83) | copy-start | bytes 98308
  76.6 19.1 %copy-start.13 = (f32[2,128,32]{2,1,0:T(8,128)}, f32[2,128,32]{2,1,0:T(8,128)S(1)}, u32[]{:S(2)}) copy-start(f32[2,128,32]{2,1,0:T(8,128)S(1)} %get-tuple-element.84) | copy-start | bytes 98308
  79.4 9.2 %copy-start.9 = (bf16[4,4,2,64,384]{4,3,2,1,0:T(8,128)(2,1)}, bf16[4,4,2,64,384]{4,3,2,1,0:T(8,128)(2,1)S(1)}, u32[]{:S(2)}) copy-start(bf16[4,4,2,64,384]{4,3,2,1,0:T(8,128)(2,1)S(1)} %slice.94) | copy-start | bytes 4718596
  79.5 9.1 %copy-start.22 = (f32[2048]{0:T(1024)}, f32[2048]{0:T(1024)S(1)}, u32[]{:S(2)}) copy-start(f32[2048]{0:T(1024)S(1)} %mul.221) | copy-start | bytes 24580
  95.5 1.6 copy-start.7
  102.6 58.6 %all-to-all-start.1 = ((bf16[8,64,1408]{2,1,0:T(8,128)(2,1)}), bf16[8,64,1408]{2,1,0:T(8,128)(2,1)S(1)}, u32[]{:S(2)}, u32[]{:S(2)}) async-start(bf16[8,64,1408]{2,1,0:T(8,128)(2,1)} %shard_map.214), calls=%async_computation.1 | async-start | bytes 2883584 | tf_op jit(solution)/shard_map/all_to_all | solution.py:707
  106.3 183.6 %all-gather.13.cloned.1.call-start = ((), (), s32[]{:S(2)}) async-start(), calls=%async_computation.14 | async-start | bytes 3932160 | tf_op jit(solution)/shard_map/all_gather | solution.py:710
  162.9 138.2 %all-gather.15.cloned.1.call-start = ((), (), s32[]{:S(2)}) async-start(), calls=%async_computation.15 | async-start | bytes 3932160 | tf_op jit(solution)/shard_map/all_gather | solution.py:710
  163.5 185.0 %all-gather.17.cloned.1.call-start = ((), (), s32[]{:S(2)}) async-start(), calls=%async_computation.16 | async-start | bytes 3604480 | tf_op jit(solution)/shard_map/all_gather | solution.py:710
  167.7 36.5 %copy-start.16 = (bf16[256,2048]{1,0:T(8,128)(2,1)S(1)}, bf16[256,2048]{1,0:T(8,128)(2,1)}, u32[]{:S(2)}) copy-start(bf16[256,2048]{1,0:T(8,128)(2,1)} %all-gather.9.cloned.1.call-done) | copy-start | bytes 3145732
  211.0 387.8 %reduce-scatter.7.cloned.1.call-start = ((), (), s32[]{:S(2)}) async-start(), calls=%async_computation.17 | async-start | bytes 2621440 | tf_op jit(solution)/shard_map/reduce_scatter | solution.py:892
  313.8 1.6 copy-start.33
  348.5 14.5 %copy-start.28 = (bf16[2048,704]{1,0:T(8,128)(2,1)S(1)}, bf16[2048,704]{1,0:T(8,128)(2,1)}, u32[]{:S(2)}) copy-start(bf16[2048,704]{1,0:T(8,128)(2,1)} %all-gather.13.cloned.1.call-done) | copy-start | bytes 8650756
  362.9 10.4 %copy-start.31 = (bf16[2048,704]{0,1:T(8,128)(2,1)}, bf16[2048,704]{0,1:T(8,128)(2,1)S(1)}, u32[]{:S(2)}) copy-start(bf16[2048,704]{0,1:T(8,128)(2,1)S(1)} %get-tuple-element.89) | copy-start | bytes 8650756
  476.6 36.5 %copy-start.29 = (bf16[704,2048]{1,0:T(8,128)(2,1)S(1)}, bf16[704,2048]{1,0:T(8,128)(2,1)}, u32[]{:S(2)}) copy-start(bf16[704,2048]{1,0:T(8,128)(2,1)} %all-gather.17.cloned.1.call-done) | copy-start | bytes 8650756
  524.0 13.1 %copy-start.32 = (bf16[2048,704]{0,1:T(8,128)(2,1)S(1)}, bf16[2048,704]{0,1:T(8,128)(2,1)}, u32[]{:S(2)}) copy-start(bf16[2048,704]{0,1:T(8,128)(2,1)} %copy-done.31) | copy-start | bytes 8650756
  524.0 138.9 %reduce-scatter.15.cloned.1.call-start = ((), (), s32[]{:S(2)}) async-start(), calls=%async_computation.21 | async-start | bytes 3604480 | tf_op jit(solution)/shard_map/reduce_scatter | solution.py:831
  537.0 144.9 %reduce-scatter.13.cloned.1.call-start = ((), (), s32[]{:S(2)}) async-start(), calls=%async_computation.20 | async-start | bytes 3604480 | tf_op jit(solution)/shard_map/reduce_scatter | solution.py:831
  547.9 0.7 copy-start.25
  547.9 0.7 copy-start.23
  547.9 192.3 %reduce-scatter.17.cloned.1.call-start = ((), (), s32[]{:S(2)}) async-start(), calls=%async_computation.22 | async-start | bytes 3604480 | tf_op jit(solution)/shard_map/reduce_scatter | solution.py:831
  548.5 221.6 %reduce-scatter.11.cloned.1.call-start = ((), (), s32[]{:S(2)}) async-start(), calls=%async_computation.19 | async-start | bytes 1310720 | tf_op jit(solution)/shard_map/reduce_scatter | solution.py:831
  557.2 41.6 %copy-start.3 = (bf16[4,2,2,128,256]{4,3,2,1,0:T(8,128)(2,1)S(1)}, bf16[4,2,2,128,256]{4,3,2,1,0:T(8,128)(2,1)}, u32[]{:S(2)}) copy-start(bf16[4,2,2,128,256]{4,3,2,1,0:T(8,128)(2,1)} %get-tuple-element.40) | copy-start | bytes 3145732
  598.8 6.9 copy-start.17
  605.7 0.9 copy-start.12
  605.7 1.0 copy-start.14
  605.7 200.5 %reduce-scatter.9.cloned.1.call-start = ((), (), s32[]{:S(2)}) async-start(), calls=%async_computation.18 | async-start | bytes 1966080 | tf_op jit(solution)/shard_map/reduce_scatter | solution.py:831
  605.8 1.5 copy-start.10
  605.8 1.8 copy-start.30
  606.6 8.1 slice-start
  607.5 7.2 slice-start.1
  614.7 6.3 copy-start.1
  614.7 6.6 copy-start.24
  662.9 6.7 copy-start.2
  665.3 18.8 %all-to-all-start.4 = ((bf16[8,64,704]{2,1,0:T(8,128)(2,1)}), bf16[8,64,704]{2,1,0:T(8,128)(2,1)}, u32[]{:S(2)}, u32[]{:S(2)}) async-start(bf16[8,64,704]{2,1,0:T(8,128)(2,1)} %bitcast.124), calls=%async_computation.9 | async-start | bytes 1572864 | tf_op jit(solution)/shard_map/all_to_all | solution.py:835
  669.6 1.6 copy-start.4
  684.2 90.3 %all-to-all-start.3 = ((bf16[8,64,704]{2,1,0:T(8,128)(2,1)}), bf16[8,64,704]{2,1,0:T(8,128)(2,1)}, u32[]{:S(2)}, u32[]{:S(2)}) async-start(bf16[8,64,704]{2,1,0:T(8,128)(2,1)} %bitcast.123), calls=%async_computation.7 | async-start | bytes 1572864 | tf_op jit(solution)/shard_map/all_to_all | solution.py:835
  774.5 2.7 copy-start.5
  774.5 37.1 %copy-start.27 = (bf16[64]{0:T(256)(128)(2,1)S(1)}, bf16[64]{0:T(256)(128)(2,1)}, u32[]{:S(2)}) copy-start(bf16[64]{0:T(256)(128)(2,1)} %param.23) | copy-start | bytes 388
  777.1 33.0 %copy-start.6 = (f32[64,5632]{1,0:T(8,128)S(1)}, f32[64,5632]{1,0:T(8,128)}, u32[]{:S(2)}) copy-start(f32[64,5632]{1,0:T(8,128)} %shard_map.221) | copy-start | bytes 4325380
  806.2 12.2 %all-to-all-start.2 = ((bf16[8,64,384]{2,1,0:T(8,128)(2,1)}), bf16[8,64,384]{2,1,0:T(8,128)(2,1)S(1)}, u32[]{:S(2)}, u32[]{:S(2)}) async-start(bf16[8,64,384]{2,1,0:T(8,128)(2,1)} %bitcast.148), calls=%async_computation.4 | async-start | bytes 786432 | tf_op jit(solution)/shard_map/all_to_all | solution.py:835
  818.8 2.7 copy-start.18
  819.1 2.5 copy-start.19
  819.1 2.3 copy-start.15
  819.1 2.4 copy-start.20
  819.1 2.4 copy-start.21
  819.2 2.6 copy-start.26
  821.4 0.8 copy-start.8
Sparse Core Ops, SparseCore 0:
  28.2 42.8 all-gather.6
  72.7 26.8 all-gather.8
  101.7 45.0 all-gather.10
  163.0 62.1 all-gather.12
  227.2 62.0 all-gather.14
  290.7 57.7 all-gather.16
  524.1 41.4 reduce-scatter.6
  567.9 55.5 reduce-scatter.14
  625.8 56.0 reduce-scatter.12
  684.1 56.0 reduce-scatter.16
  743.0 27.0 reduce-scatter.10
  772.3 33.9 reduce-scatter.8
